TPU v7x, 512 devices: a whole 4x4x16 slice. The times are simulated.
512 devices in a mesh: band: 16 (over z), ga: 32 (over y, x, core).
Axes of the slice: x: 4, y: 4, z: 16, core: 2. Of those that a mesh axis runs over, the one named last changes fastest.
Arguments:
- waves: bfloat16 [2, 512, 32768], P(None, 'band', 'ga'), may hold values from -6 to 6
- occupations: float32 [512], P('band'), may hold values from 0.000390625 to 0.0078125
- beta_table: float32 [72, 32768], P(None, 'ga'), may hold values from -0.0234375 to 0.0234375
- wave_miller: int32 [3, 32768], P(None, 'ga'), may hold values from 0 to 223
- atom_kinds: int32 [256], replicated, may hold values from 0 to 3
- atom_sites: int32 [3, 256], replicated, may hold values from 0 to 223
- aug_table: bfloat16 [684, 917504], P(None, ('band', 'ga')), may hold values from -0.00015258789 to 0.00015258789
- stick_columns: int32 [4096], P(('band', 'ga')), may hold values from -1 to 3599, as said below
Outputs:
- density: float32 [2, 224, 240, 240], P(None, 'ga', 'band')
Inputs may be any that keep to these rules, and one draw needn't show every extreme that they name: `stick_columns`: entry t is a slot of the device at place t // 8 in band-major order, of band index t // 256. -1 marks an empty slot; otherwise the entry c names the column x = (t // 256) * 15 + c // 240, y = c mod 240. Live columns of one band index are distinct. On each device the live slots come first and at least one is live; in each band index some device has all 8 slots live.
All inputs are finite; a program needn't handle non-finite values.
Results may differ from a plain program's by a relative error of at most 0.0035.
Values sent between devices are 32-bit elements; how exact they have to be, the bound alone decides.
No kernel may reach another device: no remote copies, remote signals or barrier semaphores. Data moves between devices by JAX's collectives and lax.ppermute only.
A program may use at most 64 MiB of HBM per device.

v0:
```python
import functools

import jax
import jax.numpy as jnp
import numpy as np
from jax import lax
from jax.experimental import pallas as pl
from jax.experimental.pallas import tpu as pltpu
from jax.sharding import PartitionSpec as P

NX = 240
NY = 240
NZ = 224
NH = 18
PAIRS = 171
SPECIES = 4
ATOMS = 256
HALF = NH // 2
F32 = jnp.float32
BF16 = jnp.bfloat16
VMEM = pltpu.VMEM
SMEM = pltpu.SMEM


def turn_polynomials():
    nodes = np.cos(np.pi * (np.arange(400) + 0.5) / 400)
    squares = 0.125 + 0.125 * nodes
    turns = np.sqrt(squares)
    sine = np.polynomial.chebyshev.Chebyshev.fit(
        squares, np.sin(2 * np.pi * turns) / turns, 6, domain=[0, 0.25]
    )
    cosine = np.polynomial.chebyshev.Chebyshev.fit(
        squares, np.cos(2 * np.pi * turns), 7, domain=[0, 0.25]
    )
    poly = np.polynomial.polynomial.Polynomial
    return (
        [float(v) for v in sine.convert(kind=poly).coef],
        [float(v) for v in cosine.convert(kind=poly).coef],
    )


SINE_TERMS, COSINE_TERMS = turn_polynomials()


def horner(terms, value):
    total = jnp.full_like(value, terms[-1])
    for term in terms[-2::-1]:
        total = total * value + term
    return total


def turn_waves(turns):
    square = turns * turns
    return horner(COSINE_TERMS, square), turns * horner(SINE_TERMS, square)


def turns_of(count, length):
    return (count - length * jnp.round(count * (1.0 / length))) * (1.0 / length)


def site_waves(site_cols, miller_rows):
    in_plane = site_cols[0] * miller_rows[0] + site_cols[1] * miller_rows[1]
    turns = turns_of(in_plane, NX) + turns_of(site_cols[2] * miller_rows[2], NZ)
    return turn_waves(turns - jnp.round(turns))


def iota(shape, dim):
    return lax.broadcasted_iota(jnp.int32, shape, dim)


def split_two(value):
    high = value.astype(BF16)
    return high, (value - high.astype(F32)).astype(BF16)


def mm(left, right):
    return jnp.dot(left, right, preferred_element_type=F32)


def mm_nt(left, right):
    return lax.dot_general(left, right, (((1,), (1,)), ((), ())), preferred_element_type=F32)


def mm_three(left, right_high, right_low):
    high, low = split_two(left)
    return mm(high, right_high) + (mm(high, right_low) + mm(low, right_high))


def as_columns(rows):
    eye = (iota((ATOMS, ATOMS), 0) == iota((ATOMS, ATOMS), 1)).astype(F32).astype(BF16)
    return mm_nt(eye, rows.astype(BF16))


def atom_columns(sites_ref, kinds_ref):
    rows = jnp.concatenate(
        [
            sites_ref[...].astype(F32),
            kinds_ref[...].astype(F32),
            jnp.zeros((4, ATOMS), F32),
        ],
        axis=0,
    )
    return as_columns(rows)


def project_kernel(waves, beta, miller, kinds, sites, out, cos_s, sin_s, radial_s, wave_s, kind_s):
    g_count = beta.shape[1]
    step = pl.program_id(0)

    @pl.when(step == 0)
    def _():
        columns = atom_columns(sites, kinds)
        kind_s[...] = jnp.broadcast_to(columns[:, 3:4], (ATOMS, 128))
        site_cols = [columns[:, d : d + 1] for d in range(3)]
        for start in range(0, g_count, 256):
            rows = [miller[d : d + 1, start : start + 256].astype(F32) for d in range(3)]
            cosine, sine = site_waves(site_cols, rows)
            cos_s[:, start : start + 256] = cosine
            sin_s[:, start : start + 256] = sine
        table = beta[...]
        first = table.astype(BF16)
        rest = table - first.astype(F32)
        second = rest.astype(BF16)
        third = (rest - second.astype(F32)).astype(BF16)
        radial_s[...] = jnp.zeros(radial_s.shape, BF16)
        radial_s[0:72] = first
        radial_s[80:152] = second
        radial_s[160:232] = third
        wave_re = waves[0].astype(F32)
        wave_im = waves[1].astype(F32)
        blank = jnp.zeros((64, g_count), F32)
        with_cos = jnp.concatenate([wave_re, wave_im], axis=0)
        with_sin = jnp.concatenate([-wave_im, wave_re], axis=0)
        wave_s[0] = jnp.concatenate([with_cos, blank], axis=0).T.astype(BF16)
        wave_s[1] = jnp.concatenate([with_sin, blank], axis=0).T.astype(BF16)
        wave_s[2] = jnp.concatenate([blank, with_cos], axis=0).T.astype(BF16)
        wave_s[3] = jnp.concatenate([blank, with_sin], axis=0).T.astype(BF16)

    lane = iota((ATOMS, 256), 1)
    table_row = jnp.where(lane >= 160, lane - 160, jnp.where(lane >= 80, lane - 80, lane))
    table_row = jnp.where(lane >= 240, -1, table_row).astype(F32)
    wanted = jnp.concatenate([kind_s[...], kind_s[...]], axis=1) * float(NH)
    total = None
    for which in range(2):
        pick = (table_row == wanted + (2 * step + which).astype(F32)).astype(F32).astype(BF16)
        for start in range(0, g_count, 256):
            span = slice(start, start + 256)
            radial = mm(pick, radial_s[:, span])
            part_cos = (radial * cos_s[:, span]).astype(BF16)
            part_sin = (radial * sin_s[:, span]).astype(BF16)
            part = mm(part_cos, wave_s[2 * which, span]) + mm(part_sin, wave_s[2 * which + 1, span])
            total = part if total is None else total + part
    out[...] = total.reshape(ATOMS // 8, 1, 8, 128)


def project(waves, beta, miller, kinds, sites):
    g_count = beta.shape[1]
    whole = lambda shape: pl.BlockSpec(shape, lambda i: (0,) * len(shape))
    return pl.pallas_call(
        project_kernel,
        grid=(HALF,),
        in_specs=[
            whole(waves.shape),
            whole(beta.shape),
            whole(miller.shape),
            whole((1, ATOMS)),
            whole(sites.shape),
        ],
        out_specs=pl.BlockSpec((ATOMS // 8, 1, 8, 128), lambda i: (0, i, 0, 0)),
        out_shape=jax.ShapeDtypeStruct((ATOMS // 8, HALF, 8, 128), F32),
        scratch_shapes=[
            VMEM((ATOMS, g_count), F32),
            VMEM((ATOMS, g_count), F32),
            VMEM((256, g_count), BF16),
            VMEM((4, g_count, 128), BF16),
            VMEM((ATOMS, 128), F32),
        ],
        name="project",
    )(waves, beta, miller, kinds.reshape(1, ATOMS), sites)


def pair_constants():
    ell = np.array([0, 0] + [1] * 6 + [2] * 10)
    first, second = np.triu_indices(NH)
    take = np.zeros((NH * 8, 256), np.float32)
    keep = np.zeros((NH, 256), np.float32)
    for p in range(PAIRS):
        take[second[p] * 8 : second[p] * 8 + 8, p] = 1.0
        keep[first[p], p] = 1.0 if first[p] == second[p] else 2.0
    lanes = np.zeros((8, 768), np.float32)
    lanes[:2] = -1.0
    for s in range(SPECIES):
        span = slice(s * PAIRS, (s + 1) * PAIRS)
        lanes[0, span] = np.arange(PAIRS)
        lanes[1, span] = s
        odd = (ell[first] + ell[second]) % 2
        lanes[2, span] = 1.0 - odd
        lanes[3, span] = -1.0 * odd
    return take, keep, lanes


def becsum_kernel(blocks, occ, take, keep, out):
    rows = []
    for pair in range(HALF):
        total = blocks[0, pair]
        for src in range(1, blocks.shape[0]):
            total = total + blocks[src, pair]
        if 1 <= pair <= 3:
            lane = iota((8, 128), 1)
            ahead = pltpu.roll(total, 96, 1)
            behind = pltpu.roll(total, 32, 1)
            total = jnp.where(lane % 64 < 32, -ahead, behind)
        elif pair >= 4:
            total = -total
        rows.append(total)
        rows.append(pltpu.roll(total, 64, 1))
    lane = iota((NH * 8, 128), 1)
    values = jnp.where(lane < 64, jnp.concatenate(rows, axis=0), 0.0)
    scaled = values * occ[...]
    square = lax.dot_general(
        scaled, values, (((1,), (1,)), ((), ())), precision=lax.Precision.HIGHEST,
        preferred_element_type=F32,
    )
    side = (NH * 8, NH * 8)
    square = jnp.where(iota(side, 0) % 8 == iota(side, 1) % 8, square, 0.0)
    high, low = split_two(square)
    lowest = (square - high.astype(F32) - low.astype(F32)).astype(BF16)
    chosen = mm(high, take[...]) + (mm(low, take[...]) + mm(lowest, take[...]))
    result = jnp.zeros((8, 256), F32)
    for i in range(NH):
        result = result + chosen[8 * i : 8 * i + 8] * keep[i : i + 1, :]
    for peer in range(out.shape[0]):
        out[peer] = result


def becsum_part(blocks, occupations, peers, take, keep):
    occ = jnp.tile(occupations, 4).reshape(1, 128)
    return pl.pallas_call(
        becsum_kernel,
        out_shape=jax.ShapeDtypeStruct((peers, 8, 256), F32),
        name="becsum",
    )(blocks, occ, jnp.asarray(take, BF16), jnp.asarray(keep))


def band_sum_kernel(parts, out):
    total = parts[0]
    for src in range(1, parts.shape[0]):
        total = total + parts[src]
    for peer in range(out.shape[0]):
        out[peer] = total


def band_sum(parts, peers):
    return pl.pallas_call(
        band_sum_kernel, out_shape=jax.ShapeDtypeStruct((peers, 8, 256), F32), name="band_sum"
    )(parts)


def augment_kernel(
    sticks, band, becsum, kinds, sites, lanes, cos_high, cos_low, sin_high, sin_low, table, out,
    weight_s, site_s, aug_s,
):
    step = pl.program_id(0)
    chunk = table.shape[1]

    @pl.when(step == 0)
    def _():
        columns = atom_columns(sites, kinds)
        for d in range(3):
            site_s[d] = jnp.broadcast_to(columns[:, d : d + 1], (ATOMS, 128))
        width = lanes.shape[1]
        spread = (iota((256, width), 0).astype(F32) == lanes[0:1, :]).astype(F32).astype(BF16)
        rounded = becsum[...].reshape(ATOMS, 256).astype(BF16)
        copies = mm(rounded, spread)
        mine = jnp.where(columns[:, 3:4] == lanes[1:2, :], copies, 0.0)
        weight_s[0:ATOMS] = (mine * lanes[2:3, :]).astype(BF16)
        weight_s[ATOMS:] = (mine * lanes[3:4, :]).astype(BF16)

    rows = table.shape[0]
    coeff = mm(weight_s[:, 0:rows], table[...])
    g_row = step * chunk + iota((1, chunk), 1)
    slot_row = jnp.zeros((1, chunk), jnp.int32)
    for slot in range(1, 8):
        slot_row = slot_row + (g_row >= slot * NZ).astype(jnp.int32)
    z_row = (g_row - slot_row * NZ).astype(F32)
    x_row = jnp.zeros((1, chunk), F32)
    y_row = jnp.zeros((1, chunk), F32)
    live_row = jnp.zeros((1, chunk), F32)
    for slot in range(8):
        column = sticks[slot]
        live = (column >= 0).astype(F32)
        column = jnp.maximum(column, 0)
        x_in_block = column // NY
        x_value = (band[0] * (NX // 16) + x_in_block).astype(F32)
        y_value = (column - x_in_block * NY).astype(F32)
        here = slot_row == slot
        x_row = jnp.where(here, x_value, x_row)
        y_row = jnp.where(here, y_value, y_row)
        live_row = jnp.where(here, live, live_row)
    reps = chunk // 128
    site_cols = [jnp.concatenate([site_s[d]] * reps, axis=1) for d in range(3)]
    cosine, sine = site_waves(site_cols, [x_row, y_row, z_row])
    amp_re = coeff[0:ATOMS]
    amp_im = coeff[ATOMS:]
    aug_re = jnp.sum(amp_re * cosine + amp_im * sine, axis=0, keepdims=True) * live_row
    aug_im = jnp.sum(amp_im * cosine - amp_re * sine, axis=0, keepdims=True) * live_row
    start = pl.multiple_of(step * chunk, chunk)
    aug_s[0:1, pl.ds(start, chunk)] = aug_re
    aug_s[1:2, pl.ds(start, chunk)] = aug_im

    @pl.when(step == pl.num_programs(0) - 1)
    def _():
        stick = [aug_s[0:1, s * NZ : (s + 1) * NZ] for s in range(8)]
        stick += [aug_s[1:2, s * NZ : (s + 1) * NZ] for s in range(8)]
        data = jnp.concatenate(stick, axis=0)
        by_cos = mm_three(data, cos_high[...], cos_low[...])
        by_sin = mm_three(data, sin_high[...], sin_low[...])
        out_re = by_cos[0:8] - by_sin[8:16]
        out_im = by_sin[0:8] + by_cos[8:16]
        sub = iota((8, 256), 0)
        x_info = jnp.zeros((8, 256), F32)
        y_info = jnp.zeros((8, 256), F32)
        for slot in range(8):
            column = jnp.maximum(sticks[slot], 0)
            x_in_block = column // NY
            x_info = jnp.where(sub == slot, x_in_block.astype(F32), x_info)
            y_info = jnp.where(sub == slot, (column - x_in_block * NY).astype(F32), y_info)
        lane = iota((8, 256), 1)
        out_re = jnp.where(lane < NZ, out_re, x_info)
        out_im = jnp.where(lane < NZ, out_im, y_info)
        turned = jnp.concatenate([out_re, out_im], axis=0).T
        out[...] = jnp.concatenate([turned[32 * j : 32 * j + 32] for j in range(8)], axis=1)


def z_tables():
    z = np.arange(NZ)
    plane = np.zeros(256, np.int64)
    plane[:NZ] = 7 * (np.arange(NZ) % 32) + np.arange(NZ) // 32
    angle = 2 * np.pi * ((z[:, None] * plane[None, :]) % NZ) / NZ
    live = (np.arange(256) < NZ)[None, :]
    return np.cos(angle) * live, np.sin(angle) * live


def halves(table):
    table = np.asarray(table, np.float32)
    high = table.astype(jnp.bfloat16)
    return jnp.asarray(high), jnp.asarray((table - high.astype(np.float32)).astype(jnp.bfloat16))


def augment(sticks, band, becsum, kinds, sites, lanes, table):
    rows, count = table.shape
    chunk = 256
    cosine, sine = z_tables()
    cos_high, cos_low = halves(cosine)
    sin_high, sin_low = halves(sine)
    whole = lambda shape: pl.BlockSpec(shape, lambda i: (0,) * len(shape))
    scalar = pl.BlockSpec(memory_space=SMEM)
    return pl.pallas_call(
        augment_kernel,
        grid=(count // chunk,),
        in_specs=[
            scalar,
            scalar,
            whole(becsum.shape),
            whole((1, ATOMS)),
            whole(sites.shape),
            whole(lanes.shape),
        ]
        + [whole((NZ, 256))] * 4
        + [pl.BlockSpec((rows, chunk), lambda i: (0, i))],
        out_specs=whole((32, 128)),
        out_shape=jax.ShapeDtypeStruct((32, 128), F32),
        scratch_shapes=[
            VMEM((2 * ATOMS, lanes.shape[1]), BF16),
            VMEM((3, ATOMS, 128), F32),
            VMEM((8, count), F32),
        ],
        name="augment",
    )(
        sticks, band, becsum, kinds.reshape(1, ATOMS), sites, jnp.asarray(lanes),
        cos_high, cos_low, sin_high, sin_low, table,
    )


def spread_constants():
    spread = np.zeros((8, 128, 256), np.float32)
    for slot in range(8):
        for j in range(8):
            for part in range(2):
                row = j * 16 + part * 8 + slot
                spread[slot, row, part * 128 + j * 16 : part * 128 + j * 16 + 16] = 1.0
    return spread


def y_kernel(values, spread, out):
    high, low = split_two(values[...].reshape(32, 128))
    parts = []
    for slot in range(8):
        parts.append(mm(high, spread[slot]) + mm(low, spread[slot]))
    wide = jnp.concatenate(parts, axis=0)
    y_col = wide[:, 240:241]
    source = jnp.where(iota((8, 256), 0) == 0, 112, 240)
    pick = (iota((8, 256), 1) == source).astype(F32).astype(BF16)
    info = mm_nt(pick, wide.astype(BF16))
    x_t = info[0:1, :]
    y_t = info[1:2, :]
    lane = iota((256, 128), 1)
    cosine, sine = turn_waves(turns_of(y_col * (lane % 16).astype(F32), NY))
    real = wide[:, 0:128]
    imag = wide[:, 128:256]
    keep = lane < 112
    new_re = jnp.where(keep, real * cosine - imag * sine, 0.0)
    new_im = jnp.where(keep, real * sine + imag * cosine, 0.0)
    right = jnp.concatenate(
        [
            jnp.concatenate([new_re, new_im], axis=1),
            jnp.concatenate([-new_im, new_re], axis=1),
        ],
        axis=0,
    )
    line = iota((256, 256), 0)
    here = (line % 16).astype(F32) == x_t
    far_cos, far_sin = turn_waves(turns_of(y_t * (line // 16).astype(F32), 16))
    left = jnp.concatenate([jnp.where(here, far_cos, 0.0), jnp.where(here, far_sin, 0.0)], axis=1)
    right_high, right_low = split_two(right)
    out[...] = mm_three(left, right_high, right_low).reshape(16, 16, 256)


def y_transform(values):
    spread = jnp.asarray(spread_constants(), BF16)
    return pl.pallas_call(
        y_kernel, out_shape=jax.ShapeDtypeStruct((16, 16, 256), F32), name="y_transform"
    )(values, spread)


def x_tables():
    row = np.arange(256)
    x_in = 15 * (row // 16) + row % 16
    x_out = np.arange(256)
    angle = 2 * np.pi * ((x_in[:, None] * x_out[None, :]) % NX) / NX
    live = (row % 16 < 15)[:, None] & (x_out < NX)[None, :]
    return np.cos(angle) * live, np.sin(angle) * live


def x_kernel(values, cos_high, cos_low, sin_high, sin_low, out):
    turned = values[...].reshape(256, 256).T
    by_cos = mm_three(turned, cos_high[...], cos_low[...])
    by_sin = mm_three(turned, sin_high[...], sin_low[...])
    real = by_cos[0:128] - by_sin[128:256]
    imag = by_sin[0:128] + by_cos[128:256]
    for j in range(7):
        out[0, j] = real[16 * j : 16 * j + 15, 0:NX]
        out[1, j] = imag[16 * j : 16 * j + 15, 0:NX]


def x_transform(values):
    cosine, sine = x_tables()
    return pl.pallas_call(
        x_kernel, out_shape=jax.ShapeDtypeStruct((2, 7, 15, NX), F32), name="x_transform"
    )(values, *halves(cosine), *halves(sine))


def exchange(value, axis):
    return lax.all_to_all(value, axis, 0, 0, tiled=True)


def on_device(
    waves, occupations, beta_table, wave_miller, atom_kinds, atom_sites, aug_table, stick_columns
):
    take, keep, lanes = pair_constants()
    bands = lax.axis_size("band")
    groups = lax.axis_size("ga")
    band = lax.axis_index("band").reshape(1)
    pieces = project(waves, beta_table, wave_miller, atom_kinds, atom_sites)
    pieces = exchange(pieces, "ga")
    part = becsum_part(pieces, occupations, bands, take, keep)
    summed = band_sum(exchange(part, "band"), groups)
    becsum = exchange(summed, "ga")
    columns = augment(stick_columns, band, becsum, atom_kinds, atom_sites, lanes, aug_table)
    planes = y_transform(exchange(columns.reshape(32, 1, 128), "ga"))
    return x_transform(exchange(planes, "band"))


def solution(mesh):
    in_specs = (
        P(None, "band", "ga"),
        P("band"),
        P(None, "ga"),
        P(None, "ga"),
        P(),
        P(),
        P(None, ("band", "ga")),
        P(("band", "ga")),
    )
    out_specs = P(None, "ga", "band", None)
    return jax.shard_map(
        on_device, mesh=mesh, in_specs=in_specs, out_specs=out_specs, check_vma=False
    )
```

profile of v0, /device:TPU:32, one launch (start us, length us, event | category | flops | bytes accessed | tf_op | source)
XLA Modules:
  0.0 144.5 jit_solution(1673279186003594279)
XLA Ops:
  0.0 19.8 %project.1 = f32[32,9,8,128]{3,2,1,0:T(8,128)} custom-call(bf16[2,32,1024]{2,1,0:T(8,128)(2,1)} %waves.1, f32[72,1024]{1,0:T(8,128)} %beta.1, s32[3,1024]{1,0:T(4,128)} %miller.1, s32[1,256]{1,0:T(1,128)} %bitcast.4, s32[3,256]{1,0:T(4,128)} %sites.3), custom_call_target="tpu_custom_call" | custom-call | tf_op jit(solution)/shard_map/project/pallas_call | solution.py:159
  19.8 0.0 copy-start.2
  19.8 7.5 %all-to-all-start = ((f32[32,9,8,128]{3,2,1,0:T(8,128)}), f32[32,9,8,128]{3,2,1,0:T(8,128)S(1)}, u32[]{:S(2)}, u32[]{:S(2)}) async-start(f32[32,9,8,128]{3,2,1,0:T(8,128)} %project.1), calls=%async_computation | async-start | bytes 2359296 | tf_op jit(solution)/shard_map/all_to_all | solution.py:464
  27.2 0.0 copy-done.2
  27.2 0.7 reshape_tile.3.occ
  27.9 18.0 %all-to-all-done.blocks = f32[32,9,8,128]{3,2,1,0:T(8,128)S(1)} async-done(((f32[32,9,8,128]{3,2,1,0:T(8,128)}), f32[32,9,8,128]{3,2,1,0:T(8,128)S(1)}, u32[]{:S(2)}, u32[]{:S(2)}) %all-to-all-start) | async-done | bytes 1179680 | tf_op jit(solution)/shard_map/all_to_all | solution.py:464
  45.9 0.0 copy-start
  45.9 1.0 copy-done
  46.9 2.7 %becsum.1 = f32[16,8,256]{2,1,0:T(8,128)} custom-call(f32[32,9,8,128]{3,2,1,0:T(8,128)} %copy-done, f32[1,128]{1,0:T(1,128)} %reshape_tile.3.occ, bf16[144,256]{1,0:T(8,128)(2,1)} %constant.30.clone.take, f32[18,256]{1,0:T(8,128)} %constant.31.clone.keep), custom_call_target="tpu_custom_call" | custom-call | tf_op jit(solution)/shard_map/becsum/pallas_call | solution.py:238
  49.6 29.2 %all_to_all.25.parts = f32[16,8,256]{2,1,0:T(8,128)} all-to-all(f32[16,8,256]{2,1,0:T(8,128)} %becsum.1), channel_id=1, replica_groups=mesh['band'=16,'ga'=32] {'band'}, dimensions={0} | all-to-all | bytes 262144 | tf_op jit(solution)/shard_map/all_to_all | solution.py:464
  78.8 1.6 %band_sum.1 = f32[32,8,256]{2,1,0:T(8,128)} custom-call(f32[16,8,256]{2,1,0:T(8,128)} %all_to_all.25.parts), custom_call_target="tpu_custom_call" | custom-call | tf_op jit(solution)/shard_map/band_sum/pallas_call | solution.py:254
  80.5 3.9 %all-to-all-start.2 = ((f32[32,8,256]{2,1,0:T(8,128)}), f32[32,8,256]{2,1,0:T(8,128)S(1)}, u32[]{:S(2)}, u32[]{:S(2)}) async-start(f32[32,8,256]{2,1,0:T(8,128)} %band_sum.1), calls=%async_computation.2 | async-start | bytes 524288 | tf_op jit(solution)/shard_map/all_to_all | solution.py:464
  84.4 8.8 %all-to-all-done.2.becsum = f32[32,8,256]{2,1,0:T(8,128)S(1)} async-done(((f32[32,8,256]{2,1,0:T(8,128)}), f32[32,8,256]{2,1,0:T(8,128)S(1)}, u32[]{:S(2)}, u32[]{:S(2)}) %all-to-all-start.2) | async-done | bytes 262176 | tf_op jit(solution)/shard_map/all_to_all | solution.py:464
  93.1 0.0 copy-start.1
  93.1 0.7 copy-done.1
  93.8 8.4 %augment.1 = f32[32,128]{1,0:T(8,128)} custom-call(s32[8]{0:T(128)} %sticks.1, s32[1]{0:T(128)} %bitcast.band, f32[32,8,256]{2,1,0:T(8,128)} %copy-done.1, s32[1,256]{1,0:T(1,128)} %bitcast.5, s32[3,256]{1,0:T(4,128)} %sites.3, f32[8,768]{1,0:T(8,128)} %constant.36.clone.lanes, bf16[224,256]{1,0:T(8,128)(2,1)} %constant.32.clone.cos_high, ...), custom_call_target="tpu_custom_call" | custom-call | tf_op jit(solution)/shard_map/augment/pallas_call | solution.py:358
  102.3 11.6 %all_to_all.26.values = f32[32,1,128]{2,1,0:T(1,128)} all-to-all(f32[32,1,128]{2,1,0:T(1,128)} %bitcast.3), channel_id=1, replica_groups=mesh['band'=16,'ga'=32] {'ga'}, dimensions={0} | all-to-all | bytes 32768 | tf_op jit(solution)/shard_map/all_to_all | solution.py:464
  113.9 2.9 %y_transform.1 = f32[16,16,256]{2,1,0:T(8,128)} custom-call(f32[32,1,128]{2,1,0:T(1,128)} %all_to_all.26.values, bf16[8,128,256]{2,1,0:T(8,128)(2,1)} %constant.37.clone.spread), custom_call_target="tpu_custom_call" | custom-call | tf_op jit(solution)/shard_map/y_transform/pallas_call | solution.py:431
  116.8 23.6 %all_to_all.27.values = f32[16,16,256]{2,1,0:T(8,128)} all-to-all(f32[16,16,256]{2,1,0:T(8,128)} %y_transform.1), channel_id=1, replica_groups=mesh['band'=16,'ga'=32] {'band'}, dimensions={0} | all-to-all | bytes 524288 | tf_op jit(solution)/shard_map/all_to_all | solution.py:464
  140.5 2.3 %x_transform.1 = f32[2,7,15,240]{3,2,1,0:T(8,128)} custom-call(f32[16,16,256]{2,1,0:T(8,128)} %all_to_all.27.values, bf16[256,256]{1,0:T(8,128)(2,1)} %constant.38.clone.cos_high, bf16[256,256]{1,0:T(8,128)(2,1)} %constant.39.clone.cos_low, bf16[256,256]{1,0:T(8,128)(2,1)} %constant.40.clone.sin_high, bf16[256,256]{1,0:T(8,128)(2,1)} %constant.41.clone.sin_low), custom_call_target="tpu_custom_call" | custom-call | tf_op jit(solution)/shard_map/x_transform/pallas_call | solution.py:458
  142.7 1.8 %copy.21 = f32[2,7,15,240]{3,0,2,1:T(2,128)} copy(f32[2,7,15,240]{3,2,1,0:T(8,128)} %x_transform.1) | data formatting | bytes 403200 | tf_op jit(solution)/shard_map/x_transform/pallas_call | solution.py:458
  (1 shorter events, 0.0 us)
Async XLA Ops:
  19.8 7.5 %copy-start.2 = (f32[32]{0:T(128)S(1)}, f32[32]{0:T(128)}, u32[]{:S(2)}) copy-start(f32[32]{0:T(128)} %param.21) | copy-start | bytes 388
  19.8 26.1 %all-to-all-start = ((f32[32,9,8,128]{3,2,1,0:T(8,128)}), f32[32,9,8,128]{3,2,1,0:T(8,128)S(1)}, u32[]{:S(2)}, u32[]{:S(2)}) async-start(f32[32,9,8,128]{3,2,1,0:T(8,128)} %project.1), calls=%async_computation | async-start | bytes 2359296 | tf_op jit(solution)/shard_map/all_to_all | solution.py:464
  45.9 1.0 copy-start
  80.5 12.7 %all-to-all-start.2 = ((f32[32,8,256]{2,1,0:T(8,128)}), f32[32,8,256]{2,1,0:T(8,128)S(1)}, u32[]{:S(2)}, u32[]{:S(2)}) async-start(f32[32,8,256]{2,1,0:T(8,128)} %band_sum.1), calls=%async_computation.2 | async-start | bytes 524288 | tf_op jit(solution)/shard_map/all_to_all | solution.py:464
  93.1 0.7 copy-start.1
where the time goes:
time: 145 us; the launch traced here: 144 us
  blocking collectives  64.5 us (44%)
  Pallas kernels  37.7 us (26%)
  waiting for transfers between devices  26.8 us (18%)
  starting transfers between devices  11.3 us (8%)
  local copies, waits for them, and re-layouts  4.19 us (3%)
    all_to_all x3, blocking collectives, exchange(): return lax.all_to_all(value, axis, 0, 0, tiled=True)  64.5 us
    all_to_all x2, waiting for transfers between devices, exchange(): return lax.all_to_all(value, axis, 0, 0, tiled=True)  26.8 us
    pallas_call x1, Pallas kernels, project(): pl.pallas_call(project_kernel, grid=(HALF,), in_specs=[whole(waves.shape)...  19.8 us
    all_to_all x2, starting transfers between devices, exchange(): return lax.all_to_all(value, axis, 0, 0, tiled=True)  11.3 us
    pallas_call x1, Pallas kernels, augment(): pl.pallas_call(augment_kernel, grid=(count // chunk,), in_specs=[scalar,...  8.45 us
    pallas_call x1, Pallas kernels, y_transform(): pl.pallas_call(y_kernel, out_shape=jax.ShapeDtypeStruct((16, 16, 256), F3...  2.93 us
  transfers between devices with their start and end apart: 2, of which 2 were waited for; matrix products, arithmetic and copies ran while one was open for 0% of the time, Pallas kernels for 0%

commit v1 on v0

--- a/solution.py
+++ b/solution.py
@@ -16,10 +16,12 @@
 SPECIES = 4
 ATOMS = 256
 HALF = NH // 2
+PAIRS_A_STEP = 3
 F32 = jnp.float32
 BF16 = jnp.bfloat16
 VMEM = pltpu.VMEM
 SMEM = pltpu.SMEM
+MIB = 1 << 20
 
 
 def turn_polynomials():
@@ -103,54 +105,46 @@
     return as_columns(rows)
 
 
-def project_kernel(waves, beta, miller, kinds, sites, out, cos_s, sin_s, radial_s, wave_s, kind_s):
+def project_kernel(waves, beta, miller, kinds, sites, out, site_s, wave_s, phi_s):
     g_count = beta.shape[1]
     step = pl.program_id(0)
 
     @pl.when(step == 0)
     def _():
-        columns = atom_columns(sites, kinds)
-        kind_s[...] = jnp.broadcast_to(columns[:, 3:4], (ATOMS, 128))
-        site_cols = [columns[:, d : d + 1] for d in range(3)]
+        site_rows = [sites[d : d + 1, :].astype(F32) for d in range(3)]
         for start in range(0, g_count, 256):
-            rows = [miller[d : d + 1, start : start + 256].astype(F32) for d in range(3)]
-            cosine, sine = site_waves(site_cols, rows)
-            cos_s[:, start : start + 256] = cosine
-            sin_s[:, start : start + 256] = sine
-        table = beta[...]
-        first = table.astype(BF16)
-        rest = table - first.astype(F32)
-        second = rest.astype(BF16)
-        third = (rest - second.astype(F32)).astype(BF16)
-        radial_s[...] = jnp.zeros(radial_s.shape, BF16)
-        radial_s[0:72] = first
-        radial_s[80:152] = second
-        radial_s[160:232] = third
-        wave_re = waves[0].astype(F32)
-        wave_im = waves[1].astype(F32)
-        blank = jnp.zeros((64, g_count), F32)
-        with_cos = jnp.concatenate([wave_re, wave_im], axis=0)
-        with_sin = jnp.concatenate([-wave_im, wave_re], axis=0)
-        wave_s[0] = jnp.concatenate([with_cos, blank], axis=0).T.astype(BF16)
-        wave_s[1] = jnp.concatenate([with_sin, blank], axis=0).T.astype(BF16)
-        wave_s[2] = jnp.concatenate([blank, with_cos], axis=0).T.astype(BF16)
-        wave_s[3] = jnp.concatenate([blank, with_sin], axis=0).T.astype(BF16)
-
-    lane = iota((ATOMS, 256), 1)
-    table_row = jnp.where(lane >= 160, lane - 160, jnp.where(lane >= 80, lane - 80, lane))
-    table_row = jnp.where(lane >= 240, -1, table_row).astype(F32)
-    wanted = jnp.concatenate([kind_s[...], kind_s[...]], axis=1) * float(NH)
-    total = None
-    for which in range(2):
-        pick = (table_row == wanted + (2 * step + which).astype(F32)).astype(F32).astype(BF16)
-        for start in range(0, g_count, 256):
-            span = slice(start, start + 256)
-            radial = mm(pick, radial_s[:, span])
-            part_cos = (radial * cos_s[:, span]).astype(BF16)
-            part_sin = (radial * sin_s[:, span]).astype(BF16)
-            part = mm(part_cos, wave_s[2 * which, span]) + mm(part_sin, wave_s[2 * which + 1, span])
-            total = part if total is None else total + part
-    out[...] = total.reshape(ATOMS // 8, 1, 8, 128)
+            rows = [miller[:, start : start + 256].astype(F32), jnp.zeros((5, 256), F32)]
+            columns = as_columns(jnp.concatenate(rows, axis=0))
+            cosine, sine = site_waves([columns[:, d : d + 1] for d in range(3)], site_rows)
+            site_s[start : start + 256, 0:ATOMS] = cosine.astype(BF16)
+            site_s[start : start + 256, ATOMS:] = sine.astype(BF16)
+        wave_s[0:32] = waves[0].astype(F32)
+        wave_s[32:64] = waves[1].astype(F32)
+
+    kind = jnp.concatenate([kinds[...], kinds[...]], axis=1)
+
+    def fill(slot, projector):
+        for species in range(SPECIES):
+            row = beta[pl.ds(species * NH + projector, 1), :]
+            phi_s[slot, species * 64 : species * 64 + 64] = (row * wave_s[...]).astype(BF16)
+
+    count = 2 * out.shape[1]
+    first = count * step
+    fill(0, first)
+    both = []
+    for index in range(count):
+        if index + 1 < count:
+            fill(index + 1, first + index + 1)
+        every = mm(phi_s[index], site_s[...])
+        mine = every[192:256]
+        for species in range(3):
+            mine = jnp.where(kind == species, every[species * 64 : species * 64 + 64], mine)
+        both.append(mine[0:32, 0:ATOMS] - mine[32:64, ATOMS:])
+        both.append(mine[32:64, 0:ATOMS] + mine[0:32, ATOMS:])
+        if index % 2:
+            turned = jnp.concatenate(both, axis=0).T
+            out[:, index // 2] = turned.reshape(ATOMS // 8, 8, 128)
+            both = []
 
 
 def project(waves, beta, miller, kinds, sites):
@@ -158,7 +152,7 @@
     whole = lambda shape: pl.BlockSpec(shape, lambda i: (0,) * len(shape))
     return pl.pallas_call(
         project_kernel,
-        grid=(HALF,),
+        grid=(HALF // PAIRS_A_STEP,),
         in_specs=[
             whole(waves.shape),
             whole(beta.shape),
@@ -166,14 +160,12 @@
             whole((1, ATOMS)),
             whole(sites.shape),
         ],
-        out_specs=pl.BlockSpec((ATOMS // 8, 1, 8, 128), lambda i: (0, i, 0, 0)),
+        out_specs=pl.BlockSpec((ATOMS // 8, PAIRS_A_STEP, 8, 128), lambda i: (0, i, 0, 0)),
         out_shape=jax.ShapeDtypeStruct((ATOMS // 8, HALF, 8, 128), F32),
         scratch_shapes=[
-            VMEM((ATOMS, g_count), F32),
-            VMEM((ATOMS, g_count), F32),
-            VMEM((256, g_count), BF16),
-            VMEM((4, g_count, 128), BF16),
-            VMEM((ATOMS, 128), F32),
+            VMEM((g_count, 2 * ATOMS), BF16),
+            VMEM((64, g_count), F32),
+            VMEM((2 * PAIRS_A_STEP, 256, g_count), BF16),
         ],
         name="project",
     )(waves, beta, miller, kinds.reshape(1, ATOMS), sites)
@@ -229,17 +221,21 @@
     result = jnp.zeros((8, 256), F32)
     for i in range(NH):
         result = result + chosen[8 * i : 8 * i + 8] * keep[i : i + 1, :]
+    tails = result[0:4, 128:256] + pltpu.roll(result[4:8, 128:256], 64, 1)
+    packed = jnp.concatenate([result[0:4, 0:128], tails, result[4:8, 0:128]], axis=1)
     for peer in range(out.shape[0]):
-        out[peer] = result
+        out[peer] = packed
 
 
 def becsum_part(blocks, occupations, peers, take, keep):
     occ = jnp.tile(occupations, 4).reshape(1, 128)
     return pl.pallas_call(
         becsum_kernel,
-        out_shape=jax.ShapeDtypeStruct((peers, 8, 256), F32),
+        in_specs=resident(4),
+        out_shape=jax.ShapeDtypeStruct((peers, 4, 384), F32),
         name="becsum",
-    )(blocks, occ, jnp.asarray(take, BF16), jnp.asarray(keep))
+        compiler_params=pltpu.CompilerParams(vmem_limit_bytes=12 * MIB),
+    )(on_chip(blocks), on_chip(occ), on_chip(jnp.asarray(take, BF16)), on_chip(jnp.asarray(keep)))
 
 
 def band_sum_kernel(parts, out):
@@ -252,32 +248,35 @@
 
 def band_sum(parts, peers):
     return pl.pallas_call(
-        band_sum_kernel, out_shape=jax.ShapeDtypeStruct((peers, 8, 256), F32), name="band_sum"
-    )(parts)
-
-
-def augment_kernel(
-    sticks, band, becsum, kinds, sites, lanes, cos_high, cos_low, sin_high, sin_low, table, out,
-    weight_s, site_s, aug_s,
-):
+        band_sum_kernel,
+        in_specs=resident(1),
+        out_shape=jax.ShapeDtypeStruct((peers, 4, 384), F32),
+        name="band_sum",
+        compiler_params=pltpu.CompilerParams(vmem_limit_bytes=8 * MIB),
+    )(on_chip(parts))
+
+
+def slot_column(sticks, slot):
+    column = jnp.maximum(sticks[slot], 0)
+    x_in_block = column // NY
+    return x_in_block, column - x_in_block * NY
+
+
+def structure_kernel(sticks, band, kinds, sites, out, kind_out, site_s):
     step = pl.program_id(0)
-    chunk = table.shape[1]
+    chunk = out.shape[2]
 
     @pl.when(step == 0)
     def _():
-        columns = atom_columns(sites, kinds)
+        line = iota((ATOMS, ATOMS), 0)
+        atom = line % 128 // 4 * 8 + line // 128 * 4 + line % 4
+        order = (iota((ATOMS, ATOMS), 1) == atom).astype(F32).astype(BF16)
+        rows = [sites[...].astype(F32), kinds[...].astype(F32), jnp.zeros((4, ATOMS), F32)]
+        columns = mm_nt(order, jnp.concatenate(rows, axis=0).astype(BF16))
         for d in range(3):
             site_s[d] = jnp.broadcast_to(columns[:, d : d + 1], (ATOMS, 128))
-        width = lanes.shape[1]
-        spread = (iota((256, width), 0).astype(F32) == lanes[0:1, :]).astype(F32).astype(BF16)
-        rounded = becsum[...].reshape(ATOMS, 256).astype(BF16)
-        copies = mm(rounded, spread)
-        mine = jnp.where(columns[:, 3:4] == lanes[1:2, :], copies, 0.0)
-        weight_s[0:ATOMS] = (mine * lanes[2:3, :]).astype(BF16)
-        weight_s[ATOMS:] = (mine * lanes[3:4, :]).astype(BF16)
-
-    rows = table.shape[0]
-    coeff = mm(weight_s[:, 0:rows], table[...])
+        kind_out[...] = jnp.broadcast_to(columns[:, 3:4], (ATOMS, 128))
+
     g_row = step * chunk + iota((1, chunk), 1)
     slot_row = jnp.zeros((1, chunk), jnp.int32)
     for slot in range(1, 8):
@@ -287,49 +286,98 @@
     y_row = jnp.zeros((1, chunk), F32)
     live_row = jnp.zeros((1, chunk), F32)
     for slot in range(8):
-        column = sticks[slot]
-        live = (column >= 0).astype(F32)
-        column = jnp.maximum(column, 0)
-        x_in_block = column // NY
-        x_value = (band[0] * (NX // 16) + x_in_block).astype(F32)
-        y_value = (column - x_in_block * NY).astype(F32)
+        x_in_block, y_value = slot_column(sticks, slot)
+        x_value = band[0] * (NX // 16) + x_in_block
         here = slot_row == slot
-        x_row = jnp.where(here, x_value, x_row)
-        y_row = jnp.where(here, y_value, y_row)
-        live_row = jnp.where(here, live, live_row)
+        x_row = jnp.where(here, x_value.astype(F32), x_row)
+        y_row = jnp.where(here, y_value.astype(F32), y_row)
+        live_row = jnp.where(here, (sticks[slot] >= 0).astype(F32), live_row)
     reps = chunk // 128
     site_cols = [jnp.concatenate([site_s[d]] * reps, axis=1) for d in range(3)]
     cosine, sine = site_waves(site_cols, [x_row, y_row, z_row])
-    amp_re = coeff[0:ATOMS]
-    amp_im = coeff[ATOMS:]
-    aug_re = jnp.sum(amp_re * cosine + amp_im * sine, axis=0, keepdims=True) * live_row
-    aug_im = jnp.sum(amp_im * cosine - amp_re * sine, axis=0, keepdims=True) * live_row
-    start = pl.multiple_of(step * chunk, chunk)
-    aug_s[0:1, pl.ds(start, chunk)] = aug_re
-    aug_s[1:2, pl.ds(start, chunk)] = aug_im
-
-    @pl.when(step == pl.num_programs(0) - 1)
-    def _():
-        stick = [aug_s[0:1, s * NZ : (s + 1) * NZ] for s in range(8)]
-        stick += [aug_s[1:2, s * NZ : (s + 1) * NZ] for s in range(8)]
-        data = jnp.concatenate(stick, axis=0)
-        by_cos = mm_three(data, cos_high[...], cos_low[...])
-        by_sin = mm_three(data, sin_high[...], sin_low[...])
-        out_re = by_cos[0:8] - by_sin[8:16]
-        out_im = by_sin[0:8] + by_cos[8:16]
-        sub = iota((8, 256), 0)
-        x_info = jnp.zeros((8, 256), F32)
-        y_info = jnp.zeros((8, 256), F32)
-        for slot in range(8):
-            column = jnp.maximum(sticks[slot], 0)
-            x_in_block = column // NY
-            x_info = jnp.where(sub == slot, x_in_block.astype(F32), x_info)
-            y_info = jnp.where(sub == slot, (column - x_in_block * NY).astype(F32), y_info)
-        lane = iota((8, 256), 1)
-        out_re = jnp.where(lane < NZ, out_re, x_info)
-        out_im = jnp.where(lane < NZ, out_im, y_info)
-        turned = jnp.concatenate([out_re, out_im], axis=0).T
-        out[...] = jnp.concatenate([turned[32 * j : 32 * j + 32] for j in range(8)], axis=1)
+    out[0] = cosine * live_row
+    out[1] = sine * live_row
+
+
+def structure(sticks, band, kinds, sites, count):
+    chunk = 256
+    whole = lambda shape: pl.BlockSpec(shape, lambda i: (0,) * len(shape))
+    scalar = pl.BlockSpec(memory_space=SMEM)
+    return pl.pallas_call(
+        structure_kernel,
+        grid=(count // chunk,),
+        in_specs=[scalar, scalar, whole((1, ATOMS)), whole(sites.shape)],
+        out_specs=[pl.BlockSpec((2, ATOMS, chunk), lambda i: (0, 0, i)), whole((ATOMS, 128))],
+        out_shape=[
+            jax.ShapeDtypeStruct((2, ATOMS, count), F32),
+            jax.ShapeDtypeStruct((ATOMS, 128), F32),
+        ],
+        scratch_shapes=[VMEM((3, ATOMS, 128), F32)],
+        cost_estimate=pl.CostEstimate(flops=60 * ATOMS * count, transcendentals=0, bytes_accessed=8 * ATOMS * count),
+        name="structure",
+    )(sticks, band, kinds.reshape(1, ATOMS), sites)
+
+
+def augment_kernel(
+    sticks, becsum, kinds, lanes, cos_high, cos_low, sin_high, sin_low, phases_far, table_far, out,
+    aug_s, phases, table, sems,
+):
+    copies = []
+    for index in range(table.shape[1] // 256):
+        span = pl.ds(index * 256, 256)
+        pair = [
+            pltpu.make_async_copy(table_far.at[:, span], table.at[:, span], sems.at[0, index]),
+            pltpu.make_async_copy(
+                phases_far.at[:, :, span], phases.at[:, :, span], sems.at[1, index]
+            ),
+        ]
+        for copy in pair:
+            copy.start()
+        copies.append(pair)
+    width = lanes.shape[1]
+    spread = (iota((256, width), 0).astype(F32) == lanes[0:1, :]).astype(F32).astype(BF16)
+    packed = becsum[...].reshape(128, 384)
+    tail = packed[:, 128:256]
+    rounded = jnp.concatenate(
+        [
+            jnp.concatenate([packed[:, 0:128], tail], axis=1),
+            jnp.concatenate([packed[:, 256:384], pltpu.roll(tail, 64, 1)], axis=1),
+        ],
+        axis=0,
+    ).astype(BF16)
+    mine = jnp.where(kinds[:, 0:1] == lanes[1:2, :], mm(rounded, spread), 0.0)
+    rows = table.shape[0]
+    even = (mine * lanes[2:3, :]).astype(BF16)[:, 0:rows]
+    odd = (mine * lanes[3:4, :]).astype(BF16)[:, 0:rows]
+    for start in range(0, table.shape[1], 256):
+        span = slice(start, start + 256)
+        for copy in copies[start // 256]:
+            copy.wait()
+        amp_re = mm(even, table[:, span])
+        amp_im = mm(odd, table[:, span])
+        cosine = phases[0, :, span]
+        sine = phases[1, :, span]
+        aug_s[0:1, span] = jnp.sum(amp_re * cosine + amp_im * sine, axis=0, keepdims=True)
+        aug_s[1:2, span] = jnp.sum(amp_im * cosine - amp_re * sine, axis=0, keepdims=True)
+    stick = [aug_s[0:1, s * NZ : (s + 1) * NZ] for s in range(8)]
+    stick += [aug_s[1:2, s * NZ : (s + 1) * NZ] for s in range(8)]
+    data = jnp.concatenate(stick, axis=0)
+    by_cos = mm_three(data, cos_high[...], cos_low[...])
+    by_sin = mm_three(data, sin_high[...], sin_low[...])
+    out_re = by_cos[0:8] - by_sin[8:16]
+    out_im = by_sin[0:8] + by_cos[8:16]
+    sub = iota((8, 256), 0)
+    x_info = jnp.zeros((8, 256), F32)
+    y_info = jnp.zeros((8, 256), F32)
+    for slot in range(8):
+        x_in_block, y_value = slot_column(sticks, slot)
+        x_info = jnp.where(sub == slot, x_in_block.astype(F32), x_info)
+        y_info = jnp.where(sub == slot, y_value.astype(F32), y_info)
+    lane = iota((8, 256), 1)
+    out_re = jnp.where(lane < NZ, out_re, x_info)
+    out_im = jnp.where(lane < NZ, out_im, y_info)
+    turned = jnp.concatenate([out_re, out_im], axis=0).T
+    out[...] = jnp.concatenate([turned[32 * j : 32 * j + 32] for j in range(8)], axis=1)
 
 
 def z_tables():
@@ -347,38 +395,25 @@
     return jnp.asarray(high), jnp.asarray((table - high.astype(np.float32)).astype(jnp.bfloat16))
 
 
-def augment(sticks, band, becsum, kinds, sites, lanes, table):
-    rows, count = table.shape
-    chunk = 256
+def augment(sticks, becsum, kinds, phases, lanes, table):
     cosine, sine = z_tables()
-    cos_high, cos_low = halves(cosine)
-    sin_high, sin_low = halves(sine)
-    whole = lambda shape: pl.BlockSpec(shape, lambda i: (0,) * len(shape))
-    scalar = pl.BlockSpec(memory_space=SMEM)
+    constants = [on_chip(c) for c in (*halves(cosine), *halves(sine))]
     return pl.pallas_call(
         augment_kernel,
-        grid=(count // chunk,),
-        in_specs=[
-            scalar,
-            scalar,
-            whole(becsum.shape),
-            whole((1, ATOMS)),
-            whole(sites.shape),
-            whole(lanes.shape),
-        ]
-        + [whole((NZ, 256))] * 4
-        + [pl.BlockSpec((rows, chunk), lambda i: (0, i))],
-        out_specs=whole((32, 128)),
+        in_specs=[pl.BlockSpec(memory_space=SMEM)]
+        + resident(7)
+        + [pl.BlockSpec(memory_space=pltpu.HBM)] * 2,
         out_shape=jax.ShapeDtypeStruct((32, 128), F32),
         scratch_shapes=[
-            VMEM((2 * ATOMS, lanes.shape[1]), BF16),
-            VMEM((3, ATOMS, 128), F32),
-            VMEM((8, count), F32),
+            VMEM((8, table.shape[1]), F32),
+            VMEM(phases.shape, F32),
+            VMEM(table.shape, BF16),
+            pltpu.SemaphoreType.DMA((2, table.shape[1] // 256)),
         ],
         name="augment",
     )(
-        sticks, band, becsum, kinds.reshape(1, ATOMS), sites, jnp.asarray(lanes),
-        cos_high, cos_low, sin_high, sin_low, table,
+        sticks, on_chip(becsum), on_chip(kinds), on_chip(jnp.asarray(lanes)), *constants, phases,
+        table,
     )
 
 
@@ -429,8 +464,12 @@
 def y_transform(values):
     spread = jnp.asarray(spread_constants(), BF16)
     return pl.pallas_call(
-        y_kernel, out_shape=jax.ShapeDtypeStruct((16, 16, 256), F32), name="y_transform"
-    )(values, spread)
+        y_kernel,
+        in_specs=resident(2),
+        out_shape=jax.ShapeDtypeStruct((16, 16, 256), F32),
+        name="y_transform",
+        compiler_params=pltpu.CompilerParams(vmem_limit_bytes=12 * MIB),
+    )(on_chip(values), on_chip(spread))
 
 
 def x_tables():
@@ -449,15 +488,29 @@
     real = by_cos[0:128] - by_sin[128:256]
     imag = by_sin[0:128] + by_cos[128:256]
     for j in range(7):
-        out[0, j] = real[16 * j : 16 * j + 15, 0:NX]
-        out[1, j] = imag[16 * j : 16 * j + 15, 0:NX]
+        out[j, :, 0, :] = real[16 * j : 16 * j + 15, 0:NX]
+        out[j, :, 1, :] = imag[16 * j : 16 * j + 15, 0:NX]
 
 
 def x_transform(values):
     cosine, sine = x_tables()
-    return pl.pallas_call(
-        x_kernel, out_shape=jax.ShapeDtypeStruct((2, 7, 15, NX), F32), name="x_transform"
-    )(values, *halves(cosine), *halves(sine))
+    constants = [on_chip(c) for c in (*halves(cosine), *halves(sine))]
+    result = pl.pallas_call(
+        x_kernel,
+        in_specs=resident(5),
+        out_shape=jax.ShapeDtypeStruct((7, 15, 2, NX), F32),
+        name="x_transform",
+        compiler_params=pltpu.CompilerParams(vmem_limit_bytes=12 * MIB),
+    )(on_chip(values), *constants)
+    return jnp.transpose(result, (2, 0, 1, 3))
+
+
+def on_chip(value):
+    return pltpu.with_memory_space_constraint(value, VMEM)
+
+
+def resident(count):
+    return [pl.BlockSpec(memory_space=VMEM)] * count
 
 
 def exchange(value, axis):
@@ -472,11 +525,14 @@
     groups = lax.axis_size("ga")
     band = lax.axis_index("band").reshape(1)
     pieces = project(waves, beta_table, wave_miller, atom_kinds, atom_sites)
+    phases, kind_columns = structure(
+        stick_columns, band, atom_kinds, atom_sites, aug_table.shape[1]
+    )
     pieces = exchange(pieces, "ga")
     part = becsum_part(pieces, occupations, bands, take, keep)
     summed = band_sum(exchange(part, "band"), groups)
     becsum = exchange(summed, "ga")
-    columns = augment(stick_columns, band, becsum, atom_kinds, atom_sites, lanes, aug_table)
+    columns = augment(stick_columns, becsum, kind_columns, phases, lanes, aug_table)
     planes = y_transform(exchange(columns.reshape(32, 1, 128), "ga"))
     return x_transform(exchange(planes, "band"))
 

time: 145 us -> 122 us (0.84)
  Pallas kernels: 37.7 us -> 25.5 us
  waiting for transfers between devices: 26.8 us -> 20.5 us
  local copies, waits for them, and re-layouts: 4.19 us -> 1.04 us
  blocking collectives: 64.5 us -> 63 us
    pallas_call x6 -> x7, Pallas kernels: 37.7 us -> 25.5 us  [the longest x1 9.43 us: project(): pl.pallas_call(project_kernel, grid=(HALF // PAIRS_A_STEP,), in_specs=[wh...]
    all_to_all x2, waiting for transfers between devices: 26.8 us -> 20.5 us  [exchange(): return lax.all_to_all(value, axis, 0, 0, tiled=True)]
    pallas_call x1 -> x0, local copies, waits for them, and re-layouts: 1.79 us -> none  [x_transform(): pl.pallas_call(x_kernel, out_shape=jax.ShapeDtypeStruct((2, 7, 15, NX), F...]
  transfers between devices with their start and end apart: 2 -> 2, of which waited for: 2 -> 2; matrix products, arithmetic and copies ran while one was open for 0% -> 0% of each run, Pallas kernels for 0% -> 5%
where the time goes in v1:
time: 122 us; the launch traced here: 121 us
  blocking collectives  63 us (52%)
  Pallas kernels  25.5 us (21%)
  waiting for transfers between devices  20.5 us (17%)
  starting transfers between devices  11.3 us (9%)
    all_to_all x3, blocking collectives, exchange(): return lax.all_to_all(value, axis, 0, 0, tiled=True)  63 us
    all_to_all x2, waiting for transfers between devices, exchange(): return lax.all_to_all(value, axis, 0, 0, tiled=True)  20.5 us
    all_to_all x2, starting transfers between devices, exchange(): return lax.all_to_all(value, axis, 0, 0, tiled=True)  11.3 us
    pallas_call x1, Pallas kernels, project(): pl.pallas_call(project_kernel, grid=(HALF // PAIRS_A_STEP,), in_specs=[wh...  9.43 us
    pallas_call x1, Pallas kernels, structure(): pl.pallas_call(structure_kernel, grid=(count // chunk,), in_specs=[scalar...  6.28 us
    pallas_call x1, Pallas kernels, augment(): pl.pallas_call(augment_kernel, in_specs=[pl.BlockSpec(memory_space=SMEM)]...  5.94 us
  transfers between devices with their start and end apart: 2, of which 2 were waited for; matrix products, arithmetic and copies ran while one was open for 0% of the time, Pallas kernels for 5%

profile of v1, /device:TPU:32, one launch (start us, length us, event | category | flops | bytes accessed | tf_op | source)
XLA Modules:
  0.0 121.5 jit_solution(10411175669812964445)
XLA Ops:
  0.0 0.0 copy-start.12
  0.0 0.0 copy-start.10
  0.0 0.0 copy-start.13
  0.0 9.4 %project.1 = f32[32,9,8,128]{3,2,1,0:T(8,128)} custom-call(bf16[2,32,1024]{2,1,0:T(8,128)(2,1)} %waves.1, f32[72,1024]{1,0:T(8,128)} %beta.1, s32[3,1024]{1,0:T(4,128)} %miller.1, s32[1,256]{1,0:T(1,128)} %bitcast.5, s32[3,256]{1,0:T(4,128)} %sites.3), custom_call_target="tpu_custom_call" | custom-call | tf_op jit(solution)/shard_map/project/pallas_call | solution.py:153
  9.4 0.0 copy-start.6
  9.4 0.0 copy-start.7
  9.4 0.0 copy-start.8
  9.4 0.0 copy-start.9
  9.5 0.0 copy-start.11
  9.5 7.5 %all-to-all-start = ((f32[32,9,8,128]{3,2,1,0:T(8,128)}), f32[32,9,8,128]{3,2,1,0:T(8,128)S(1)}, u32[]{:S(2)}, u32[]{:S(2)}) async-start(f32[32,9,8,128]{3,2,1,0:T(8,128)} %project.1), calls=%async_computation | async-start | bytes 2359296 | tf_op jit(solution)/shard_map/all_to_all | solution.py:517
  17.0 0.0 copy-done.13
  17.0 0.1 reshape_tile.3.occ
  17.1 18.6 %all-to-all-done.blocks = f32[32,9,8,128]{3,2,1,0:T(8,128)S(1)} async-done(((f32[32,9,8,128]{3,2,1,0:T(8,128)}), f32[32,9,8,128]{3,2,1,0:T(8,128)S(1)}, u32[]{:S(2)}, u32[]{:S(2)}) %all-to-all-start) | async-done | bytes 1179680 | tf_op jit(solution)/shard_map/all_to_all | solution.py:517
  35.6 0.0 copy-done.12
  35.6 0.0 copy-done.10
  35.6 0.8 becsum.1
  36.5 28.2 %all_to_all.25.parts = f32[16,4,384]{2,1,0:T(4,128)S(1)} all-to-all(f32[16,4,384]{2,1,0:T(4,128)S(1)} %becsum.1), channel_id=1, replica_groups=mesh['band'=16,'ga'=32] {'band'}, dimensions={0} | all-to-all | bytes 196608 | tf_op jit(solution)/shard_map/all_to_all | solution.py:517
  64.7 0.7 band_sum.1
  65.4 3.9 %all-to-all-start.2 = ((f32[32,4,384]{2,1,0:T(4,128)}), f32[32,4,384]{2,1,0:T(4,128)S(1)}, u32[]{:S(2)}, u32[]{:S(2)}) async-start(f32[32,4,384]{2,1,0:T(4,128)} %band_sum.1), calls=%async_computation.2 | async-start | bytes 393216 | tf_op jit(solution)/shard_map/all_to_all | solution.py:517
  69.3 6.3 %structure.1 = (f32[2,256,1792]{2,1,0:T(8,128)}, f32[256,128]{1,0:T(8,128)}) custom-call(s32[8]{0:T(128)} %sticks.3, s32[1]{0:T(128)} %bitcast.1.band, s32[1,256]{1,0:T(1,128)} %bitcast.6, s32[3,256]{1,0:T(4,128)} %sites.3), custom_call_target="tpu_custom_call" | custom-call | flops 27525120 | bytes 3670016 | tf_op jit(solution)/shard_map/structure/pallas_call | solution.py:306
  75.5 1.9 %all-to-all-done.2.becsum = f32[32,4,384]{2,1,0:T(4,128)S(1)} async-done(((f32[32,4,384]{2,1,0:T(4,128)}), f32[32,4,384]{2,1,0:T(4,128)S(1)}, u32[]{:S(2)}, u32[]{:S(2)}) %all-to-all-start.2) | async-done | bytes 196640 | tf_op jit(solution)/shard_map/all_to_all | solution.py:517
  77.4 0.0 copy-done.6
  77.4 0.0 copy-done.7
  77.4 0.0 copy-done.8
  77.4 0.0 copy-done.9
  77.4 0.0 copy-done.11
  77.4 0.0 copy-start.5
  77.5 0.9 copy-done.5
  78.4 0.0 copy-start
  78.4 0.0 copy-start.1
  78.4 0.0 copy-start.2
  78.4 0.0 copy-start.3
  78.4 0.0 copy-start.4
  78.4 5.9 %augment.1 = f32[32,128]{1,0:T(8,128)} custom-call(s32[8]{0:T(128)} %sticks.3, f32[32,4,384]{2,1,0:T(4,128)S(1)} %all-to-all-done.2.becsum, f32[256,128]{1,0:T(8,128)S(1)} %copy-done.5, f32[8,768]{1,0:T(8,128)S(1)} %copy-done.11, bf16[224,256]{1,0:T(8,128)(2,1)S(1)} %copy-done.9, bf16[224,256]{1,0:T(8,128)(2,1)S(1)} %copy-done.8, ...), custom_call_target="tpu_custom_call" | custom-call | tf_op jit(solution)/shard_map/augment/pallas_call | solution.py:401
  84.3 12.8 %all_to_all.26.values = f32[32,1,128]{2,1,0:T(1,128)S(1)} all-to-all(f32[32,1,128]{2,1,0:T(1,128)} %bitcast.4), channel_id=1, replica_groups=mesh['band'=16,'ga'=32] {'ga'}, dimensions={0} | all-to-all | bytes 32768 | tf_op jit(solution)/shard_map/all_to_all | solution.py:517
  97.2 0.0 copy-done
  97.2 1.2 y_transform.1
  98.3 22.0 %all_to_all.27.values = f32[16,16,256]{2,1,0:T(8,128)S(1)} all-to-all(f32[16,16,256]{2,1,0:T(8,128)S(1)} %y_transform.1), channel_id=1, replica_groups=mesh['band'=16,'ga'=32] {'band'}, dimensions={0} | all-to-all | bytes 524288 | tf_op jit(solution)/shard_map/all_to_all | solution.py:517
  120.3 0.0 copy-done.1
  120.3 0.0 copy-done.2
  120.3 0.0 copy-done.3
  120.3 0.0 copy-done.4
  120.3 1.2 x_transform.1
  (1 shorter events, 0.0 us)
Async XLA Ops:
  0.0 35.6 %copy-start.12 = (f32[18,256]{1,0:T(8,128)S(1)}, f32[18,256]{1,0:T(8,128)}, u32[]{:S(2)}) copy-start(f32[18,256]{1,0:T(8,128)} %constant.31.clone.keep) | copy-start | bytes 55300
  0.0 35.6 %copy-start.10 = (bf16[144,256]{1,0:T(8,128)(2,1)S(1)}, bf16[144,256]{1,0:T(8,128)(2,1)}, u32[]{:S(2)}) copy-start(bf16[144,256]{1,0:T(8,128)(2,1)} %constant.30.clone.take) | copy-start | bytes 221188
  0.0 16.9 %copy-start.13 = (f32[32]{0:T(128)S(1)}, f32[32]{0:T(128)}, u32[]{:S(2)}) copy-start(f32[32]{0:T(128)} %param.21) | copy-start | bytes 388
  9.4 68.0 %copy-start.6 = (bf16[224,256]{1,0:T(8,128)(2,1)S(1)}, bf16[224,256]{1,0:T(8,128)(2,1)}, u32[]{:S(2)}) copy-start(bf16[224,256]{1,0:T(8,128)(2,1)} %constant.35.clone.sin_low) | copy-start | bytes 344068
  9.4 68.0 %copy-start.7 = (bf16[224,256]{1,0:T(8,128)(2,1)S(1)}, bf16[224,256]{1,0:T(8,128)(2,1)}, u32[]{:S(2)}) copy-start(bf16[224,256]{1,0:T(8,128)(2,1)} %constant.34.clone.sin_high) | copy-start | bytes 344068
  9.4 68.0 %copy-start.8 = (bf16[224,256]{1,0:T(8,128)(2,1)S(1)}, bf16[224,256]{1,0:T(8,128)(2,1)}, u32[]{:S(2)}) copy-start(bf16[224,256]{1,0:T(8,128)(2,1)} %constant.33.clone.cos_low) | copy-start | bytes 344068
  9.4 68.0 %copy-start.9 = (bf16[224,256]{1,0:T(8,128)(2,1)S(1)}, bf16[224,256]{1,0:T(8,128)(2,1)}, u32[]{:S(2)}) copy-start(bf16[224,256]{1,0:T(8,128)(2,1)} %constant.32.clone.cos_high) | copy-start | bytes 344068
  9.5 68.0 %copy-start.11 = (f32[8,768]{1,0:T(8,128)S(1)}, f32[8,768]{1,0:T(8,128)}, u32[]{:S(2)}) copy-start(f32[8,768]{1,0:T(8,128)} %constant.36.clone.lanes) | copy-start | bytes 73732
  9.5 26.2 %all-to-all-start = ((f32[32,9,8,128]{3,2,1,0:T(8,128)}), f32[32,9,8,128]{3,2,1,0:T(8,128)S(1)}, u32[]{:S(2)}, u32[]{:S(2)}) async-start(f32[32,9,8,128]{3,2,1,0:T(8,128)} %project.1), calls=%async_computation | async-start | bytes 2359296 | tf_op jit(solution)/shard_map/all_to_all | solution.py:517
  65.4 12.0 %all-to-all-start.2 = ((f32[32,4,384]{2,1,0:T(4,128)}), f32[32,4,384]{2,1,0:T(4,128)S(1)}, u32[]{:S(2)}, u32[]{:S(2)}) async-start(f32[32,4,384]{2,1,0:T(4,128)} %band_sum.1), calls=%async_computation.2 | async-start | bytes 393216 | tf_op jit(solution)/shard_map/all_to_all | solution.py:517
  77.4 0.9 copy-start.5
  78.4 18.8 %copy-start = (bf16[8,128,256]{2,1,0:T(8,128)(2,1)S(1)}, bf16[8,128,256]{2,1,0:T(8,128)(2,1)}, u32[]{:S(2)}) copy-start(bf16[8,128,256]{2,1,0:T(8,128)(2,1)} %constant.37.clone.spread) | copy-start | bytes 1572868
  78.4 42.0 %copy-start.1 = (bf16[256,256]{1,0:T(8,128)(2,1)S(1)}, bf16[256,256]{1,0:T(8,128)(2,1)}, u32[]{:S(2)}) copy-start(bf16[256,256]{1,0:T(8,128)(2,1)} %constant.41.clone.sin_low) | copy-start | bytes 393220
  78.4 42.0 %copy-start.2 = (bf16[256,256]{1,0:T(8,128)(2,1)S(1)}, bf16[256,256]{1,0:T(8,128)(2,1)}, u32[]{:S(2)}) copy-start(bf16[256,256]{1,0:T(8,128)(2,1)} %constant.40.clone.sin_high) | copy-start | bytes 393220
  78.4 42.0 %copy-start.3 = (bf16[256,256]{1,0:T(8,128)(2,1)S(1)}, bf16[256,256]{1,0:T(8,128)(2,1)}, u32[]{:S(2)}) copy-start(bf16[256,256]{1,0:T(8,128)(2,1)} %constant.39.clone.cos_low) | copy-start | bytes 393220
  78.4 42.0 %copy-start.4 = (bf16[256,256]{1,0:T(8,128)(2,1)S(1)}, bf16[256,256]{1,0:T(8,128)(2,1)}, u32[]{:S(2)}) copy-start(bf16[256,256]{1,0:T(8,128)(2,1)} %constant.38.clone.cos_high) | copy-start | bytes 393220

commit v2 on v1

--- a/solution.py
+++ b/solution.py
@@ -1,4 +1,4 @@
-import functools
+import math
 
 import jax
 import jax.numpy as jnp
@@ -22,6 +22,7 @@
 VMEM = pltpu.VMEM
 SMEM = pltpu.SMEM
 MIB = 1 << 20
+AHEAD = 7
 
 
 def turn_polynomials():
@@ -32,7 +33,7 @@
         squares, np.sin(2 * np.pi * turns) / turns, 6, domain=[0, 0.25]
     )
     cosine = np.polynomial.chebyshev.Chebyshev.fit(
-        squares, np.cos(2 * np.pi * turns), 7, domain=[0, 0.25]
+        squares, np.cos(2 * np.pi * turns), 6, domain=[0, 0.25]
     )
     poly = np.polynomial.polynomial.Polynomial
     return (
@@ -61,9 +62,10 @@
 
 
 def site_waves(site_cols, miller_rows):
-    in_plane = site_cols[0] * miller_rows[0] + site_cols[1] * miller_rows[1]
-    turns = turns_of(in_plane, NX) + turns_of(site_cols[2] * miller_rows[2], NZ)
-    return turn_waves(turns - jnp.round(turns))
+    parts = math.lcm(NX, NY, NZ)
+    rows = [row * (parts // length) for row, length in zip(miller_rows, (NX, NY, NZ))]
+    count = site_cols[0] * rows[0] + site_cols[1] * rows[1] + site_cols[2] * rows[2]
+    return turn_waves(turns_of(count, parts))
 
 
 def iota(shape, dim):
@@ -93,58 +95,82 @@
     return mm_nt(eye, rows.astype(BF16))
 
 
-def atom_columns(sites_ref, kinds_ref):
-    rows = jnp.concatenate(
-        [
-            sites_ref[...].astype(F32),
-            kinds_ref[...].astype(F32),
-            jnp.zeros((4, ATOMS), F32),
-        ],
-        axis=0,
-    )
-    return as_columns(rows)
-
-
-def project_kernel(waves, beta, miller, kinds, sites, out, site_s, wave_s, phi_s):
+def species_order(sites, kinds, places):
+    kind_row = kinds[...].astype(F32)
+    every = [sites[...].astype(F32), kind_row, jnp.zeros((4, ATOMS), F32)]
+    every = jnp.concatenate(every, axis=0).astype(BF16)
+    eye = (iota((ATOMS, ATOMS), 0) == iota((ATOMS, ATOMS), 1)).astype(F32).astype(BF16)
+    kind_col = mm_nt(eye, every)[:, 3:4]
+    earlier = iota((ATOMS, ATOMS), 0) < iota((ATOMS, ATOMS), 1)
+    ahead = (kind_col < kind_row) | ((kind_col == kind_row) & earlier)
+    rank = jnp.sum(ahead.astype(F32), axis=0, keepdims=True)
+    return every, (places.astype(F32) == rank).astype(F32).astype(BF16)
+
+
+def project_kernel(
+    waves, beta, miller, kinds, sites, out, kind_s, site_s, wave_s, phi_s, sum_s, entry_s
+):
     g_count = beta.shape[1]
+    half = ATOMS // 2
     step = pl.program_id(0)
 
     @pl.when(step == 0)
     def _():
-        site_rows = [sites[d : d + 1, :].astype(F32) for d in range(3)]
+        below = jnp.int32(0)
+        last = jnp.int32(0)
+        for species in range(SPECIES - 1):
+            below = below + jnp.sum((kinds[...] == species).astype(jnp.int32))
+            last = last + (below < half).astype(jnp.int32)
+        for entry in range(SPECIES + 1):
+            later = (entry > last).astype(jnp.int32)
+            entry_s[0, entry] = entry - later
+            entry_s[1, entry] = later
+        every, order = species_order(sites, kinds, iota((ATOMS, ATOMS), 0))
+        mine = mm_nt(every, order)
+        for part in range(2):
+            span = slice(part * half, part * half + half)
+            kind_s[part, 0:1, 0:half] = mine[3:4, span]
+            kind_s[part, 0:1, half:] = mine[3:4, span]
+        site_rows = [mine[d : d + 1] for d in range(3)]
         for start in range(0, g_count, 256):
             rows = [miller[:, start : start + 256].astype(F32), jnp.zeros((5, 256), F32)]
             columns = as_columns(jnp.concatenate(rows, axis=0))
             cosine, sine = site_waves([columns[:, d : d + 1] for d in range(3)], site_rows)
-            site_s[start : start + 256, 0:ATOMS] = cosine.astype(BF16)
-            site_s[start : start + 256, ATOMS:] = sine.astype(BF16)
+            for part in range(2):
+                span = slice(part * half, part * half + half)
+                site_s[part, start : start + 256, 0:half] = cosine[:, span].astype(BF16)
+                site_s[part, start : start + 256, half:] = sine[:, span].astype(BF16)
         wave_s[0:32] = waves[0].astype(F32)
         wave_s[32:64] = waves[1].astype(F32)
 
-    kind = jnp.concatenate([kinds[...], kinds[...]], axis=1)
-
-    def fill(slot, projector):
-        for species in range(SPECIES):
-            row = beta[pl.ds(species * NH + projector, 1), :]
-            phi_s[slot, species * 64 : species * 64 + 64] = (row * wave_s[...]).astype(BF16)
-
     count = 2 * out.shape[1]
-    first = count * step
-    fill(0, first)
-    both = []
-    for index in range(count):
-        if index + 1 < count:
-            fill(index + 1, first + index + 1)
-        every = mm(phi_s[index], site_s[...])
-        mine = every[192:256]
-        for species in range(3):
-            mine = jnp.where(kind == species, every[species * 64 : species * 64 + 64], mine)
-        both.append(mine[0:32, 0:ATOMS] - mine[32:64, ATOMS:])
-        both.append(mine[32:64, 0:ATOMS] + mine[0:32, ATOMS:])
-        if index % 2:
+
+    def fill(entry):
+        first = entry_s[0, entry] * NH + count * step
+        for index in range(count):
+            row = beta[pl.ds(first + index, 1), :]
+            phi_s[entry, 64 * index : 64 * index + 64] = (row * wave_s[...]).astype(BF16)
+
+    fill(0)
+    for entry in range(SPECIES + 1):
+        if entry < SPECIES:
+            fill(entry + 1)
+        part = entry_s[1, entry]
+        every = mm(phi_s[entry], site_s[part])
+        members = kind_s[part, 0:1, :] == entry_s[0, entry].astype(F32)
+        sum_s[part] = jnp.where(members, every, sum_s[part])
+
+    for index in range(0, count, 2):
+        for part in range(2):
+            both = []
+            for which in range(index, index + 2):
+                real = sum_s[part, 64 * which : 64 * which + 32, :]
+                imag = sum_s[part, 64 * which + 32 : 64 * which + 64, :]
+                both.append(real[:, 0:half] - imag[:, half:])
+                both.append(imag[:, 0:half] + real[:, half:])
             turned = jnp.concatenate(both, axis=0).T
-            out[:, index // 2] = turned.reshape(ATOMS // 8, 8, 128)
-            both = []
+            span = slice(part * half // 8, (part + 1) * half // 8)
+            out[span, index // 2] = turned.reshape(half // 8, 8, 128)
 
 
 def project(waves, beta, miller, kinds, sites):
@@ -163,9 +189,12 @@
         out_specs=pl.BlockSpec((ATOMS // 8, PAIRS_A_STEP, 8, 128), lambda i: (0, i, 0, 0)),
         out_shape=jax.ShapeDtypeStruct((ATOMS // 8, HALF, 8, 128), F32),
         scratch_shapes=[
-            VMEM((g_count, 2 * ATOMS), BF16),
+            VMEM((2, 8, ATOMS), F32),
+            VMEM((2, g_count, ATOMS), BF16),
             VMEM((64, g_count), F32),
-            VMEM((2 * PAIRS_A_STEP, 256, g_count), BF16),
+            VMEM((SPECIES + 1, 128 * PAIRS_A_STEP, g_count), BF16),
+            VMEM((2, 128 * PAIRS_A_STEP, ATOMS), F32),
+            SMEM((2, SPECIES + 1), jnp.int32),
         ],
         name="project",
     )(waves, beta, miller, kinds.reshape(1, ATOMS), sites)
@@ -269,10 +298,9 @@
     @pl.when(step == 0)
     def _():
         line = iota((ATOMS, ATOMS), 0)
-        atom = line % 128 // 4 * 8 + line // 128 * 4 + line % 4
-        order = (iota((ATOMS, ATOMS), 1) == atom).astype(F32).astype(BF16)
-        rows = [sites[...].astype(F32), kinds[...].astype(F32), jnp.zeros((4, ATOMS), F32)]
-        columns = mm_nt(order, jnp.concatenate(rows, axis=0).astype(BF16))
+        places = line % 128 // 4 * 8 + line // 128 * 4 + line % 4
+        every, order = species_order(sites, kinds, places)
+        columns = mm_nt(order, every)
         for d in range(3):
             site_s[d] = jnp.broadcast_to(columns[:, d : d + 1], (ATOMS, 128))
         kind_out[...] = jnp.broadcast_to(columns[:, 3:4], (ATOMS, 128))
@@ -307,10 +335,13 @@
         structure_kernel,
         grid=(count // chunk,),
         in_specs=[scalar, scalar, whole((1, ATOMS)), whole(sites.shape)],
-        out_specs=[pl.BlockSpec((2, ATOMS, chunk), lambda i: (0, 0, i)), whole((ATOMS, 128))],
+        out_specs=[
+            pl.BlockSpec((2, ATOMS, chunk), lambda i: (0, 0, i)),
+            pl.BlockSpec(memory_space=VMEM),
+        ],
         out_shape=[
             jax.ShapeDtypeStruct((2, ATOMS, count), F32),
-            jax.ShapeDtypeStruct((ATOMS, 128), F32),
+            VMEM((ATOMS, 128), F32),
         ],
         scratch_shapes=[VMEM((3, ATOMS, 128), F32)],
         cost_estimate=pl.CostEstimate(flops=60 * ATOMS * count, transcendentals=0, bytes_accessed=8 * ATOMS * count),
@@ -319,21 +350,23 @@
 
 
 def augment_kernel(
-    sticks, becsum, kinds, lanes, cos_high, cos_low, sin_high, sin_low, phases_far, table_far, out,
-    aug_s, phases, table, sems,
+    sticks, becsum, kinds, lanes, cos_high, cos_low, sin_high, sin_low, phases_far,
+    table_far, out, aug_s, phases, table, sems,
 ):
     copies = []
     for index in range(table.shape[1] // 256):
         span = pl.ds(index * 256, 256)
-        pair = [
-            pltpu.make_async_copy(table_far.at[:, span], table.at[:, span], sems.at[0, index]),
-            pltpu.make_async_copy(
-                phases_far.at[:, :, span], phases.at[:, :, span], sems.at[1, index]
-            ),
-        ]
-        for copy in pair:
+        copies.append(
+            [
+                pltpu.make_async_copy(table_far.at[:, span], table.at[:, span], sems.at[0, index]),
+                pltpu.make_async_copy(
+                    phases_far.at[:, :, span], phases.at[:, :, span], sems.at[1, index]
+                ),
+            ]
+        )
+    for needed in copies[0:AHEAD]:
+        for copy in needed:
             copy.start()
-        copies.append(pair)
     width = lanes.shape[1]
     spread = (iota((256, width), 0).astype(F32) == lanes[0:1, :]).astype(F32).astype(BF16)
     packed = becsum[...].reshape(128, 384)
@@ -351,6 +384,9 @@
     odd = (mine * lanes[3:4, :]).astype(BF16)[:, 0:rows]
     for start in range(0, table.shape[1], 256):
         span = slice(start, start + 256)
+        if start // 256 + AHEAD < len(copies):
+            for copy in copies[start // 256 + AHEAD]:
+                copy.start()
         for copy in copies[start // 256]:
             copy.wait()
         amp_re = mm(even, table[:, span])
@@ -528,6 +564,7 @@
     phases, kind_columns = structure(
         stick_columns, band, atom_kinds, atom_sites, aug_table.shape[1]
     )
+    occupations, phases = lax.optimization_barrier((occupations, phases))
     pieces = exchange(pieces, "ga")
     part = becsum_part(pieces, occupations, bands, take, keep)
     summed = band_sum(exchange(part, "band"), groups)

time: 122 us -> 117 us (0.959)
  blocking collectives: 63 us -> 73.2 us
  waiting for transfers between devices: 20.5 us -> 12.3 us
  starting transfers between devices: 11.3 us -> 7.47 us
  Pallas kernels: 25.5 us -> 23.5 us
    all_to_all x3 -> x4, blocking collectives: 63 us -> 73.2 us  [exchange(): return lax.all_to_all(value, axis, 0, 0, tiled=True)]
    all_to_all x2 -> x1, waiting for transfers between devices: 20.5 us -> 12.3 us  [exchange(): return lax.all_to_all(value, axis, 0, 0, tiled=True)]
    all_to_all x2 -> x1, starting transfers between devices: 11.3 us -> 7.47 us  [exchange(): return lax.all_to_all(value, axis, 0, 0, tiled=True)]
    pallas_call x1, Pallas kernels: 9.43 us -> 8.07 us  [project(): pl.pallas_call(project_kernel, grid=(HALF // PAIRS_A_STEP,), in_specs=[wh...]
  transfers between devices with their start and end apart: 2 -> 1, of which waited for: 2 -> 1; matrix products, arithmetic and copies ran while one was open for 0% -> 0% of each run, Pallas kernels for 5% -> 5%
where the time goes in v2:
time: 117 us
  blocking collectives  73.2 us (63%)
  Pallas kernels  23.5 us (20%)
  waiting for transfers between devices  12.3 us (11%)
  starting transfers between devices  7.47 us (6%)
    all_to_all x4, blocking collectives, exchange(): return lax.all_to_all(value, axis, 0, 0, tiled=True)  73.2 us
    all_to_all x1, waiting for transfers between devices, exchange(): return lax.all_to_all(value, axis, 0, 0, tiled=True)  12.3 us
    pallas_call x1, Pallas kernels, project(): pl.pallas_call(project_kernel, grid=(HALF // PAIRS_A_STEP,), in_specs=[wh...  8.07 us
    all_to_all x1, starting transfers between devices, exchange(): return lax.all_to_all(value, axis, 0, 0, tiled=True)  7.47 us
    pallas_call x1, Pallas kernels, structure(): pl.pallas_call(structure_kernel, grid=(count // chunk,), in_specs=[scalar...  6.34 us
    pallas_call x1, Pallas kernels, augment(): pl.pallas_call(augment_kernel, in_specs=[pl.BlockSpec(memory_space=SMEM)]...  5.94 us
  transfers between devices with their start and end apart: 1, of which 1 were waited for; matrix products, arithmetic and copies ran while one was open for 0% of the time, Pallas kernels for 5%

profile of v2, /device:TPU:32, one launch (start us, length us, event | category | flops | bytes accessed | tf_op | source)
XLA Modules:
  0.0 116.7 jit_solution(5243653012493454819)
XLA Ops:
  0.0 0.0 copy-start.11
  0.0 0.0 copy-start.9
  0.0 0.0 copy-start.12
  0.0 8.1 %project.1 = f32[32,9,8,128]{3,2,1,0:T(8,128)} custom-call(bf16[2,32,1024]{2,1,0:T(8,128)(2,1)} %waves.1, f32[72,1024]{1,0:T(8,128)} %beta.1, s32[3,1024]{1,0:T(4,128)} %miller.1, s32[1,256]{1,0:T(1,128)} %bitcast.5, s32[3,256]{1,0:T(4,128)} %sites.3), custom_call_target="tpu_custom_call" | custom-call | tf_op jit(solution)/shard_map/project/pallas_call | solution.py:179
  8.1 0.0 copy-start.5
  8.1 0.0 copy-start.6
  8.1 0.0 copy-start.7
  8.1 0.0 copy-start.8
  8.1 0.0 copy-start.10
  8.1 7.5 %all-to-all-start = ((f32[32,9,8,128]{3,2,1,0:T(8,128)}), f32[32,9,8,128]{3,2,1,0:T(8,128)S(1)}, u32[]{:S(2)}, u32[]{:S(2)}) async-start(f32[32,9,8,128]{3,2,1,0:T(8,128)} %project.1), calls=%async_computation | async-start | bytes 2359296 | tf_op jit(solution)/shard_map/all_to_all | solution.py:553
  15.6 6.3 %structure.1 = (f32[2,256,1792]{2,1,0:T(8,128)}, f32[256,128]{1,0:T(8,128)S(1)}) custom-call(s32[8]{0:T(128)} %sticks.3, s32[1]{0:T(128)} %bitcast.1.band, s32[1,256]{1,0:T(1,128)} %bitcast.6, s32[3,256]{1,0:T(4,128)} %sites.3), custom_call_target="tpu_custom_call" | custom-call | flops 27525120 | bytes 3670016 | tf_op jit(solution)/shard_map/structure/pallas_call | solution.py:334
  21.9 0.0 copy-done.12
  21.9 0.1 reshape_tile.3.occ
  22.0 12.3 %all-to-all-done.blocks = f32[32,9,8,128]{3,2,1,0:T(8,128)S(1)} async-done(((f32[32,9,8,128]{3,2,1,0:T(8,128)}), f32[32,9,8,128]{3,2,1,0:T(8,128)S(1)}, u32[]{:S(2)}, u32[]{:S(2)}) %all-to-all-start) | async-done | bytes 1179680 | tf_op jit(solution)/shard_map/all_to_all | solution.py:553
  34.3 0.0 copy-done.11
  34.3 0.0 copy-done.9
  34.3 0.8 becsum.1
  35.1 28.2 %all_to_all.25.parts = f32[16,4,384]{2,1,0:T(4,128)S(1)} all-to-all(f32[16,4,384]{2,1,0:T(4,128)S(1)} %becsum.1), channel_id=1, replica_groups=mesh['band'=16,'ga'=32] {'band'}, dimensions={0} | all-to-all | bytes 196608 | tf_op jit(solution)/shard_map/all_to_all | solution.py:553
  63.4 11.4 %all_to_all.26.becsum = f32[32,4,384]{2,1,0:T(4,128)S(1)} all-to-all(f32[32,4,384]{2,1,0:T(4,128)S(1)} %band_sum.1), channel_id=1, replica_groups=mesh['band'=16,'ga'=32] {'ga'}, dimensions={0} | all-to-all | bytes 393216 | tf_op jit(solution)/shard_map/all_to_all | solution.py:553
  74.7 0.0 copy-done.5
  74.7 0.0 copy-done.6
  74.7 0.0 copy-done.7
  74.7 0.0 copy-done.8
  74.8 0.0 copy-done.10
  74.8 0.0 copy-start
  74.8 0.0 copy-start.1
  74.8 0.0 copy-start.2
  74.8 0.0 copy-start.3
  74.8 0.0 copy-start.4
  74.8 5.9 %augment.1 = f32[32,128]{1,0:T(8,128)} custom-call(s32[8]{0:T(128)} %sticks.3, f32[32,4,384]{2,1,0:T(4,128)S(1)} %all_to_all.26.becsum, f32[256,128]{1,0:T(8,128)S(1)} %get-tuple-element.11.kinds, f32[8,768]{1,0:T(8,128)S(1)} %copy-done.10, bf16[224,256]{1,0:T(8,128)(2,1)S(1)} %copy-done.8, bf16[224,256]{1,0:T(8,128)(2,1)S(1)} %copy-done.7, ...), custom_call_target="tpu_custom_call" | custom-call | tf_op jit(solution)/shard_map/augment/pallas_call | solution.py:437
  80.8 11.2 %all_to_all.27.values = f32[32,1,128]{2,1,0:T(1,128)S(1)} all-to-all(f32[32,1,128]{2,1,0:T(1,128)} %bitcast.4), channel_id=1, replica_groups=mesh['band'=16,'ga'=32] {'ga'}, dimensions={0} | all-to-all | bytes 32768 | tf_op jit(solution)/shard_map/all_to_all | solution.py:553
  92.0 0.0 copy-done
  92.0 1.1 y_transform.1
  93.1 22.4 %all_to_all.28.values = f32[16,16,256]{2,1,0:T(8,128)S(1)} all-to-all(f32[16,16,256]{2,1,0:T(8,128)S(1)} %y_transform.1), channel_id=1, replica_groups=mesh['band'=16,'ga'=32] {'band'}, dimensions={0} | all-to-all | bytes 524288 | tf_op jit(solution)/shard_map/all_to_all | solution.py:553
  115.5 0.0 copy-done.1
  115.5 0.0 copy-done.2
  115.5 0.0 copy-done.3
  115.5 0.0 copy-done.4
  115.5 1.2 x_transform.1
  (2 shorter events, 0.0 us)
Async XLA Ops:
  0.0 34.3 %copy-start.11 = (f32[18,256]{1,0:T(8,128)S(1)}, f32[18,256]{1,0:T(8,128)}, u32[]{:S(2)}) copy-start(f32[18,256]{1,0:T(8,128)} %constant.31.clone.keep) | copy-start | bytes 55300
  0.0 34.3 %copy-start.9 = (bf16[144,256]{1,0:T(8,128)(2,1)S(1)}, bf16[144,256]{1,0:T(8,128)(2,1)}, u32[]{:S(2)}) copy-start(bf16[144,256]{1,0:T(8,128)(2,1)} %constant.30.clone.take) | copy-start | bytes 221188
  0.0 21.9 %copy-start.12 = (f32[32]{0:T(128)S(1)}, f32[32]{0:T(128)}, u32[]{:S(2)}) copy-start(f32[32]{0:T(128)} %param.21) | copy-start | bytes 388
  8.1 66.7 %copy-start.5 = (bf16[224,256]{1,0:T(8,128)(2,1)S(1)}, bf16[224,256]{1,0:T(8,128)(2,1)}, u32[]{:S(2)}) copy-start(bf16[224,256]{1,0:T(8,128)(2,1)} %constant.35.clone.sin_low) | copy-start | bytes 344068
  8.1 66.7 %copy-start.6 = (bf16[224,256]{1,0:T(8,128)(2,1)S(1)}, bf16[224,256]{1,0:T(8,128)(2,1)}, u32[]{:S(2)}) copy-start(bf16[224,256]{1,0:T(8,128)(2,1)} %constant.34.clone.sin_high) | copy-start | bytes 344068
  8.1 66.7 %copy-start.7 = (bf16[224,256]{1,0:T(8,128)(2,1)S(1)}, bf16[224,256]{1,0:T(8,128)(2,1)}, u32[]{:S(2)}) copy-start(bf16[224,256]{1,0:T(8,128)(2,1)} %constant.33.clone.cos_low) | copy-start | bytes 344068
  8.1 66.7 %copy-start.8 = (bf16[224,256]{1,0:T(8,128)(2,1)S(1)}, bf16[224,256]{1,0:T(8,128)(2,1)}, u32[]{:S(2)}) copy-start(bf16[224,256]{1,0:T(8,128)(2,1)} %constant.32.clone.cos_high) | copy-start | bytes 344068
  8.1 66.7 %copy-start.10 = (f32[8,768]{1,0:T(8,128)S(1)}, f32[8,768]{1,0:T(8,128)}, u32[]{:S(2)}) copy-start(f32[8,768]{1,0:T(8,128)} %constant.36.clone.lanes) | copy-start | bytes 73732
  8.1 26.2 %all-to-all-start = ((f32[32,9,8,128]{3,2,1,0:T(8,128)}), f32[32,9,8,128]{3,2,1,0:T(8,128)S(1)}, u32[]{:S(2)}, u32[]{:S(2)}) async-start(f32[32,9,8,128]{3,2,1,0:T(8,128)} %project.1), calls=%async_computation | async-start | bytes 2359296 | tf_op jit(solution)/shard_map/all_to_all | solution.py:553
  74.8 17.2 %copy-start = (bf16[8,128,256]{2,1,0:T(8,128)(2,1)S(1)}, bf16[8,128,256]{2,1,0:T(8,128)(2,1)}, u32[]{:S(2)}) copy-start(bf16[8,128,256]{2,1,0:T(8,128)(2,1)} %constant.37.clone.spread) | copy-start | bytes 1572868
  74.8 40.7 %copy-start.1 = (bf16[256,256]{1,0:T(8,128)(2,1)S(1)}, bf16[256,256]{1,0:T(8,128)(2,1)}, u32[]{:S(2)}) copy-start(bf16[256,256]{1,0:T(8,128)(2,1)} %constant.41.clone.sin_low) | copy-start | bytes 393220
  74.8 40.7 %copy-start.2 = (bf16[256,256]{1,0:T(8,128)(2,1)S(1)}, bf16[256,256]{1,0:T(8,128)(2,1)}, u32[]{:S(2)}) copy-start(bf16[256,256]{1,0:T(8,128)(2,1)} %constant.40.clone.sin_high) | copy-start | bytes 393220
  74.8 40.7 %copy-start.3 = (bf16[256,256]{1,0:T(8,128)(2,1)S(1)}, bf16[256,256]{1,0:T(8,128)(2,1)}, u32[]{:S(2)}) copy-start(bf16[256,256]{1,0:T(8,128)(2,1)} %constant.39.clone.cos_low) | copy-start | bytes 393220
  74.8 40.7 %copy-start.4 = (bf16[256,256]{1,0:T(8,128)(2,1)S(1)}, bf16[256,256]{1,0:T(8,128)(2,1)}, u32[]{:S(2)}) copy-start(bf16[256,256]{1,0:T(8,128)(2,1)} %constant.38.clone.cos_high) | copy-start | bytes 393220

commit v3 on v2

--- a/solution.py
+++ b/solution.py
@@ -22,7 +22,7 @@
 VMEM = pltpu.VMEM
 SMEM = pltpu.SMEM
 MIB = 1 << 20
-AHEAD = 7
+NEAR = 2
 
 
 def turn_polynomials():
@@ -108,14 +108,21 @@
 
 
 def project_kernel(
-    waves, beta, miller, kinds, sites, out, kind_s, site_s, wave_s, phi_s, sum_s, entry_s
+    waves_far, beta_far, miller, kinds, sites, out, kind_s, site_s, wave_s, phi_s, sum_s, entry_s,
+    waves, beta, sems,
 ):
     g_count = beta.shape[1]
     half = ATOMS // 2
     step = pl.program_id(0)
+    loads = [
+        pltpu.make_async_copy(waves_far, waves, sems.at[0]),
+        pltpu.make_async_copy(beta_far, beta, sems.at[1]),
+    ]
 
     @pl.when(step == 0)
     def _():
+        for load in loads:
+            load.start()
         below = jnp.int32(0)
         last = jnp.int32(0)
         for species in range(SPECIES - 1):
@@ -140,6 +147,8 @@
                 span = slice(part * half, part * half + half)
                 site_s[part, start : start + 256, 0:half] = cosine[:, span].astype(BF16)
                 site_s[part, start : start + 256, half:] = sine[:, span].astype(BF16)
+        for load in loads:
+            load.wait()
         wave_s[0:32] = waves[0].astype(F32)
         wave_s[32:64] = waves[1].astype(F32)
 
@@ -180,8 +189,8 @@
         project_kernel,
         grid=(HALF // PAIRS_A_STEP,),
         in_specs=[
-            whole(waves.shape),
-            whole(beta.shape),
+            pl.BlockSpec(memory_space=pltpu.HBM),
+            pl.BlockSpec(memory_space=pltpu.HBM),
             whole(miller.shape),
             whole((1, ATOMS)),
             whole(sites.shape),
@@ -195,6 +204,9 @@
             VMEM((SPECIES + 1, 128 * PAIRS_A_STEP, g_count), BF16),
             VMEM((2, 128 * PAIRS_A_STEP, ATOMS), F32),
             SMEM((2, SPECIES + 1), jnp.int32),
+            VMEM(waves.shape, BF16),
+            VMEM(beta.shape, F32),
+            pltpu.SemaphoreType.DMA((2,)),
         ],
         name="project",
     )(waves, beta, miller, kinds.reshape(1, ATOMS), sites)
@@ -291,21 +303,8 @@
     return x_in_block, column - x_in_block * NY
 
 
-def structure_kernel(sticks, band, kinds, sites, out, kind_out, site_s):
-    step = pl.program_id(0)
-    chunk = out.shape[2]
-
-    @pl.when(step == 0)
-    def _():
-        line = iota((ATOMS, ATOMS), 0)
-        places = line % 128 // 4 * 8 + line // 128 * 4 + line % 4
-        every, order = species_order(sites, kinds, places)
-        columns = mm_nt(order, every)
-        for d in range(3):
-            site_s[d] = jnp.broadcast_to(columns[:, d : d + 1], (ATOMS, 128))
-        kind_out[...] = jnp.broadcast_to(columns[:, 3:4], (ATOMS, 128))
-
-    g_row = step * chunk + iota((1, chunk), 1)
+def column_waves(sticks, band, site_cols, first, chunk):
+    g_row = first + iota((1, chunk), 1)
     slot_row = jnp.zeros((1, chunk), jnp.int32)
     for slot in range(1, 8):
         slot_row = slot_row + (g_row >= slot * NZ).astype(jnp.int32)
@@ -320,15 +319,33 @@
         x_row = jnp.where(here, x_value.astype(F32), x_row)
         y_row = jnp.where(here, y_value.astype(F32), y_row)
         live_row = jnp.where(here, (sticks[slot] >= 0).astype(F32), live_row)
-    reps = chunk // 128
-    site_cols = [jnp.concatenate([site_s[d]] * reps, axis=1) for d in range(3)]
     cosine, sine = site_waves(site_cols, [x_row, y_row, z_row])
-    out[0] = cosine * live_row
-    out[1] = sine * live_row
+    return cosine * live_row, sine * live_row
+
+
+def structure_kernel(sticks, band, kinds, sites, out, atoms_out, site_s):
+    step = pl.program_id(0)
+    chunk = out.shape[2]
+
+    @pl.when(step == 0)
+    def _():
+        line = iota((ATOMS, ATOMS), 0)
+        places = line % 128 // 4 * 8 + line // 128 * 4 + line % 4
+        every, order = species_order(sites, kinds, places)
+        columns = mm_nt(order, every)
+        for d in range(3):
+            site_s[d] = jnp.broadcast_to(columns[:, d : d + 1], (ATOMS, chunk))
+        atoms_out[...] = jnp.concatenate([columns, jnp.zeros((ATOMS, 120), F32)], axis=1)
+
+    site_cols = [site_s[d] for d in range(3)]
+    cosine, sine = column_waves(sticks, band, site_cols, (step + NEAR) * chunk, chunk)
+    out[0] = cosine
+    out[1] = sine
 
 
 def structure(sticks, band, kinds, sites, count):
     chunk = 256
+    count = count - NEAR * chunk
     whole = lambda shape: pl.BlockSpec(shape, lambda i: (0,) * len(shape))
     scalar = pl.BlockSpec(memory_space=SMEM)
     return pl.pallas_call(
@@ -343,30 +360,37 @@
             jax.ShapeDtypeStruct((2, ATOMS, count), F32),
             VMEM((ATOMS, 128), F32),
         ],
-        scratch_shapes=[VMEM((3, ATOMS, 128), F32)],
-        cost_estimate=pl.CostEstimate(flops=60 * ATOMS * count, transcendentals=0, bytes_accessed=8 * ATOMS * count),
+        scratch_shapes=[VMEM((3, ATOMS, chunk), F32)],
+        cost_estimate=pl.CostEstimate(
+            flops=60 * ATOMS * count, transcendentals=0, bytes_accessed=8 * ATOMS * count
+        ),
         name="structure",
     )(sticks, band, kinds.reshape(1, ATOMS), sites)
 
 
 def augment_kernel(
-    sticks, becsum, kinds, lanes, cos_high, cos_low, sin_high, sin_low, phases_far,
+    sticks, band, becsum, atoms, lanes, cos_high, cos_low, sin_high, sin_low, phases_far,
     table_far, out, aug_s, phases, table, sems,
 ):
     copies = []
     for index in range(table.shape[1] // 256):
         span = pl.ds(index * 256, 256)
-        copies.append(
-            [
-                pltpu.make_async_copy(table_far.at[:, span], table.at[:, span], sems.at[0, index]),
-                pltpu.make_async_copy(
-                    phases_far.at[:, :, span], phases.at[:, :, span], sems.at[1, index]
-                ),
-            ]
-        )
-    for needed in copies[0:AHEAD]:
+        needed = [
+            pltpu.make_async_copy(table_far.at[:, span], table.at[:, span], sems.at[0, index])
+        ]
+        if index >= NEAR:
+            here = pl.ds((index - NEAR) * 256, 256)
+            needed.append(
+                pltpu.make_async_copy(phases_far.at[:, :, here], phases.at[:, :, span], sems.at[1, index])
+            )
         for copy in needed:
             copy.start()
+        copies.append(needed)
+    site_cols = [jnp.broadcast_to(atoms[:, d : d + 1], (ATOMS, 256)) for d in range(3)]
+    for start in range(0, NEAR * 256, 256):
+        cosine, sine = column_waves(sticks, band, site_cols, start, 256)
+        phases[0, :, start : start + 256] = cosine
+        phases[1, :, start : start + 256] = sine
     width = lanes.shape[1]
     spread = (iota((256, width), 0).astype(F32) == lanes[0:1, :]).astype(F32).astype(BF16)
     packed = becsum[...].reshape(128, 384)
@@ -378,15 +402,12 @@
         ],
         axis=0,
     ).astype(BF16)
-    mine = jnp.where(kinds[:, 0:1] == lanes[1:2, :], mm(rounded, spread), 0.0)
+    mine = jnp.where(atoms[:, 3:4] == lanes[1:2, :], mm(rounded, spread), 0.0)
     rows = table.shape[0]
     even = (mine * lanes[2:3, :]).astype(BF16)[:, 0:rows]
     odd = (mine * lanes[3:4, :]).astype(BF16)[:, 0:rows]
     for start in range(0, table.shape[1], 256):
         span = slice(start, start + 256)
-        if start // 256 + AHEAD < len(copies):
-            for copy in copies[start // 256 + AHEAD]:
-                copy.start()
         for copy in copies[start // 256]:
             copy.wait()
         amp_re = mm(even, table[:, span])
@@ -431,24 +452,24 @@
     return jnp.asarray(high), jnp.asarray((table - high.astype(np.float32)).astype(jnp.bfloat16))
 
 
-def augment(sticks, becsum, kinds, phases, lanes, table):
+def augment(sticks, band, becsum, atoms, phases, lanes, table):
     cosine, sine = z_tables()
     constants = [on_chip(c) for c in (*halves(cosine), *halves(sine))]
     return pl.pallas_call(
         augment_kernel,
-        in_specs=[pl.BlockSpec(memory_space=SMEM)]
+        in_specs=[pl.BlockSpec(memory_space=SMEM)] * 2
         + resident(7)
         + [pl.BlockSpec(memory_space=pltpu.HBM)] * 2,
         out_shape=jax.ShapeDtypeStruct((32, 128), F32),
         scratch_shapes=[
             VMEM((8, table.shape[1]), F32),
-            VMEM(phases.shape, F32),
+            VMEM((2, ATOMS, table.shape[1]), F32),
             VMEM(table.shape, BF16),
             pltpu.SemaphoreType.DMA((2, table.shape[1] // 256)),
         ],
         name="augment",
     )(
-        sticks, on_chip(becsum), on_chip(kinds), on_chip(jnp.asarray(lanes)), *constants, phases,
+        sticks, band, on_chip(becsum), on_chip(atoms), on_chip(jnp.asarray(lanes)), *constants, phases,
         table,
     )
 
@@ -561,7 +582,7 @@
     groups = lax.axis_size("ga")
     band = lax.axis_index("band").reshape(1)
     pieces = project(waves, beta_table, wave_miller, atom_kinds, atom_sites)
-    phases, kind_columns = structure(
+    phases, atoms = structure(
         stick_columns, band, atom_kinds, atom_sites, aug_table.shape[1]
     )
     occupations, phases = lax.optimization_barrier((occupations, phases))
@@ -569,7 +590,7 @@
     part = becsum_part(pieces, occupations, bands, take, keep)
     summed = band_sum(exchange(part, "band"), groups)
     becsum = exchange(summed, "ga")
-    columns = augment(stick_columns, becsum, kind_columns, phases, lanes, aug_table)
+    columns = augment(stick_columns, band, becsum, atoms, phases, lanes, aug_table)
     planes = y_transform(exchange(columns.reshape(32, 1, 128), "ga"))
     return x_transform(exchange(planes, "band"))
 

time: 117 us -> 117 us (level)
  Pallas kernels: 23.5 us -> 21.7 us
  waiting for transfers between devices: 12.3 us -> 13.6 us
    pallas_call x1, Pallas kernels: 6.34 us -> 5.04 us  [structure(): pl.pallas_call(structure_kernel, grid=(count // chunk,), in_specs=[scalar...]
    all_to_all x1, waiting for transfers between devices: 12.3 us -> 13.6 us  [exchange(): return lax.all_to_all(value, axis, 0, 0, tiled=True)]
  transfers between devices with their start and end apart: 1 -> 1, of which waited for: 1 -> 1; matrix products, arithmetic and copies ran while one was open for 0% -> 0% of each run, Pallas kernels for 5% -> 4%
where the time goes in v3:
time: 117 us; the launch traced here: 116 us
  blocking collectives  73.2 us (63%)
  Pallas kernels  21.7 us (19%)
  waiting for transfers between devices  13.6 us (12%)
  starting transfers between devices  7.47 us (6%)
    all_to_all x4, blocking collectives, exchange(): return lax.all_to_all(value, axis, 0, 0, tiled=True)  73.2 us
    all_to_all x1, waiting for transfers between devices, exchange(): return lax.all_to_all(value, axis, 0, 0, tiled=True)  13.6 us
    pallas_call x1, Pallas kernels, project(): pl.pallas_call(project_kernel, grid=(HALF // PAIRS_A_STEP,), in_specs=[pl...  7.76 us
    all_to_all x1, starting transfers between devices, exchange(): return lax.all_to_all(value, axis, 0, 0, tiled=True)  7.47 us
    pallas_call x1, Pallas kernels, augment(): pl.pallas_call(augment_kernel, in_specs=[pl.BlockSpec(memory_space=SMEM)]...  5.76 us
    pallas_call x1, Pallas kernels, structure(): pl.pallas_call(structure_kernel, grid=(count // chunk,), in_specs=[scalar...  5.04 us
  transfers between devices with their start and end apart: 1, of which 1 were waited for; matrix products, arithmetic and copies ran while one was open for 0% of the time, Pallas kernels for 4%

profile of v3, /device:TPU:32, one launch (start us, length us, event | category | flops | bytes accessed | tf_op | source)
XLA Modules:
  0.0 116.3 jit_solution(9552950748107271903)
XLA Ops:
  0.0 0.0 copy-start.11
  0.0 0.0 copy-start.9
  0.0 0.0 copy-start.12
  0.0 7.8 %project.1 = f32[32,9,8,128]{3,2,1,0:T(8,128)} custom-call(bf16[2,32,1024]{2,1,0:T(8,128)(2,1)} %waves_far.1, f32[72,1024]{1,0:T(8,128)} %beta_far.1, s32[3,1024]{1,0:T(4,128)} %miller.1, s32[1,256]{1,0:T(1,128)} %bitcast.5, s32[3,256]{1,0:T(4,128)} %sites.3), custom_call_target="tpu_custom_call" | custom-call | tf_op jit(solution)/shard_map/project/pallas_call | solution.py:188
  7.8 0.0 copy-start.5
  7.8 0.0 copy-start.6
  7.8 0.0 copy-start.7
  7.8 0.0 copy-start.8
  7.8 0.0 copy-start.10
  7.8 7.5 %all-to-all-start = ((f32[32,9,8,128]{3,2,1,0:T(8,128)}), f32[32,9,8,128]{3,2,1,0:T(8,128)S(1)}, u32[]{:S(2)}, u32[]{:S(2)}) async-start(f32[32,9,8,128]{3,2,1,0:T(8,128)} %project.1), calls=%async_computation | async-start | bytes 2359296 | tf_op jit(solution)/shard_map/all_to_all | solution.py:574
  15.3 5.0 %structure.1 = (f32[2,256,1280]{2,1,0:T(8,128)}, f32[256,128]{1,0:T(8,128)S(1)}) custom-call(s32[8]{0:T(128)} %sticks.3, s32[1]{0:T(128)} %bitcast.band, s32[1,256]{1,0:T(1,128)} %bitcast.6, s32[3,256]{1,0:T(4,128)} %sites.3), custom_call_target="tpu_custom_call" | custom-call | flops 19660800 | bytes 2621440 | tf_op jit(solution)/shard_map/structure/pallas_call | solution.py:351
  20.4 0.0 copy-done.12
  20.4 0.1 reshape_tile.3.occ
  20.5 13.6 %all-to-all-done.blocks = f32[32,9,8,128]{3,2,1,0:T(8,128)S(1)} async-done(((f32[32,9,8,128]{3,2,1,0:T(8,128)}), f32[32,9,8,128]{3,2,1,0:T(8,128)S(1)}, u32[]{:S(2)}, u32[]{:S(2)}) %all-to-all-start) | async-done | bytes 1179680 | tf_op jit(solution)/shard_map/all_to_all | solution.py:574
  34.0 0.0 copy-done.11
  34.0 0.0 copy-done.9
  34.0 0.8 becsum.1
  34.8 28.2 %all_to_all.25.parts = f32[16,4,384]{2,1,0:T(4,128)S(1)} all-to-all(f32[16,4,384]{2,1,0:T(4,128)S(1)} %becsum.1), channel_id=1, replica_groups=mesh['band'=16,'ga'=32] {'band'}, dimensions={0} | all-to-all | bytes 196608 | tf_op jit(solution)/shard_map/all_to_all | solution.py:574
  63.1 11.4 %all_to_all.26.becsum = f32[32,4,384]{2,1,0:T(4,128)S(1)} all-to-all(f32[32,4,384]{2,1,0:T(4,128)S(1)} %band_sum.1), channel_id=1, replica_groups=mesh['band'=16,'ga'=32] {'ga'}, dimensions={0} | all-to-all | bytes 393216 | tf_op jit(solution)/shard_map/all_to_all | solution.py:574
  74.5 0.0 copy-done.5
  74.5 0.0 copy-done.6
  74.5 0.0 copy-done.7
  74.5 0.0 copy-done.8
  74.5 0.0 copy-done.10
  74.5 0.0 copy-start
  74.5 0.0 copy-start.1
  74.5 0.0 copy-start.2
  74.5 0.0 copy-start.3
  74.6 0.0 copy-start.4
  74.6 5.8 %augment.1 = f32[32,128]{1,0:T(8,128)} custom-call(s32[8]{0:T(128)} %sticks.3, s32[1]{0:T(128)} %bitcast.band, f32[32,4,384]{2,1,0:T(4,128)S(1)} %all_to_all.26.becsum, f32[256,128]{1,0:T(8,128)S(1)} %get-tuple-element.11.atoms, f32[8,768]{1,0:T(8,128)S(1)} %copy-done.10, bf16[224,256]{1,0:T(8,128)(2,1)S(1)} %copy-done.8, bf16[224,256]{1,0:T(8,128)(2,1)S(1)} %copy-done.7, ...), custom_call_target="tpu_custom_call" | custom-call | tf_op jit(solution)/shard_map/augment/pallas_call | solution.py:458
  80.3 11.2 %all_to_all.27.values = f32[32,1,128]{2,1,0:T(1,128)S(1)} all-to-all(f32[32,1,128]{2,1,0:T(1,128)} %bitcast.4), channel_id=1, replica_groups=mesh['band'=16,'ga'=32] {'ga'}, dimensions={0} | all-to-all | bytes 32768 | tf_op jit(solution)/shard_map/all_to_all | solution.py:574
  91.5 0.0 copy-done
  91.5 1.1 y_transform.1
  92.7 22.4 %all_to_all.28.values = f32[16,16,256]{2,1,0:T(8,128)S(1)} all-to-all(f32[16,16,256]{2,1,0:T(8,128)S(1)} %y_transform.1), channel_id=1, replica_groups=mesh['band'=16,'ga'=32] {'band'}, dimensions={0} | all-to-all | bytes 524288 | tf_op jit(solution)/shard_map/all_to_all | solution.py:574
  115.1 0.0 copy-done.1
  115.1 0.0 copy-done.2
  115.1 0.0 copy-done.3
  115.1 0.0 copy-done.4
  115.1 1.2 x_transform.1
  (2 shorter events, 0.0 us)
Async XLA Ops:
  0.0 34.0 %copy-start.11 = (f32[18,256]{1,0:T(8,128)S(1)}, f32[18,256]{1,0:T(8,128)}, u32[]{:S(2)}) copy-start(f32[18,256]{1,0:T(8,128)} %constant.31.clone.keep) | copy-start | bytes 55300
  0.0 34.0 %copy-start.9 = (bf16[144,256]{1,0:T(8,128)(2,1)S(1)}, bf16[144,256]{1,0:T(8,128)(2,1)}, u32[]{:S(2)}) copy-start(bf16[144,256]{1,0:T(8,128)(2,1)} %constant.30.clone.take) | copy-start | bytes 221188
  0.0 20.4 %copy-start.12 = (f32[32]{0:T(128)S(1)}, f32[32]{0:T(128)}, u32[]{:S(2)}) copy-start(f32[32]{0:T(128)} %param.21) | copy-start | bytes 388
  7.8 66.7 %copy-start.5 = (bf16[224,256]{1,0:T(8,128)(2,1)S(1)}, bf16[224,256]{1,0:T(8,128)(2,1)}, u32[]{:S(2)}) copy-start(bf16[224,256]{1,0:T(8,128)(2,1)} %constant.35.clone.sin_low) | copy-start | bytes 344068
  7.8 66.7 %copy-start.6 = (bf16[224,256]{1,0:T(8,128)(2,1)S(1)}, bf16[224,256]{1,0:T(8,128)(2,1)}, u32[]{:S(2)}) copy-start(bf16[224,256]{1,0:T(8,128)(2,1)} %constant.34.clone.sin_high) | copy-start | bytes 344068
  7.8 66.7 %copy-start.7 = (bf16[224,256]{1,0:T(8,128)(2,1)S(1)}, bf16[224,256]{1,0:T(8,128)(2,1)}, u32[]{:S(2)}) copy-start(bf16[224,256]{1,0:T(8,128)(2,1)} %constant.33.clone.cos_low) | copy-start | bytes 344068
  7.8 66.7 %copy-start.8 = (bf16[224,256]{1,0:T(8,128)(2,1)S(1)}, bf16[224,256]{1,0:T(8,128)(2,1)}, u32[]{:S(2)}) copy-start(bf16[224,256]{1,0:T(8,128)(2,1)} %constant.32.clone.cos_high) | copy-start | bytes 344068
  7.8 66.7 %copy-start.10 = (f32[8,768]{1,0:T(8,128)S(1)}, f32[8,768]{1,0:T(8,128)}, u32[]{:S(2)}) copy-start(f32[8,768]{1,0:T(8,128)} %constant.36.clone.lanes) | copy-start | bytes 73732
  7.8 26.2 %all-to-all-start = ((f32[32,9,8,128]{3,2,1,0:T(8,128)}), f32[32,9,8,128]{3,2,1,0:T(8,128)S(1)}, u32[]{:S(2)}, u32[]{:S(2)}) async-start(f32[32,9,8,128]{3,2,1,0:T(8,128)} %project.1), calls=%async_computation | async-start | bytes 2359296 | tf_op jit(solution)/shard_map/all_to_all | solution.py:574
  74.5 17.0 %copy-start = (bf16[8,128,256]{2,1,0:T(8,128)(2,1)S(1)}, bf16[8,128,256]{2,1,0:T(8,128)(2,1)}, u32[]{:S(2)}) copy-start(bf16[8,128,256]{2,1,0:T(8,128)(2,1)} %constant.37.clone.spread) | copy-start | bytes 1572868
  74.5 40.6 %copy-start.1 = (bf16[256,256]{1,0:T(8,128)(2,1)S(1)}, bf16[256,256]{1,0:T(8,128)(2,1)}, u32[]{:S(2)}) copy-start(bf16[256,256]{1,0:T(8,128)(2,1)} %constant.41.clone.sin_low) | copy-start | bytes 393220
  74.5 40.6 %copy-start.2 = (bf16[256,256]{1,0:T(8,128)(2,1)S(1)}, bf16[256,256]{1,0:T(8,128)(2,1)}, u32[]{:S(2)}) copy-start(bf16[256,256]{1,0:T(8,128)(2,1)} %constant.40.clone.sin_high) | copy-start | bytes 393220
  74.5 40.5 %copy-start.3 = (bf16[256,256]{1,0:T(8,128)(2,1)S(1)}, bf16[256,256]{1,0:T(8,128)(2,1)}, u32[]{:S(2)}) copy-start(bf16[256,256]{1,0:T(8,128)(2,1)} %constant.39.clone.cos_low) | copy-start | bytes 393220
  74.6 40.5 %copy-start.4 = (bf16[256,256]{1,0:T(8,128)(2,1)S(1)}, bf16[256,256]{1,0:T(8,128)(2,1)}, u32[]{:S(2)}) copy-start(bf16[256,256]{1,0:T(8,128)(2,1)} %constant.38.clone.cos_high) | copy-start | bytes 393220
